TPU v7x, 32 devices: a whole 2x2x4 slice. The times are simulated.
32 devices in a mesh: owner: 4 (over z), rows: 8 (over y, x, core).
Axes of the slice: x: 2, y: 2, z: 4, core: 2. Of those that a mesh axis runs over, the one named last changes fastest.
Arguments:
- w_gate: float32 [128, 2048, 768], P('owner', 'rows'), may hold values from -0.1875 to 0.1875
- w_up: float32 [128, 2048, 768], P('owner', 'rows'), may hold values from -0.1875 to 0.1875
- router_weight: float32 [2048, 128], P('rows', 'owner'), may hold values from -0.125 to 0.125
- router_gain: float32 [2048], P('rows'), may hold values from 0.25 to 1.75
Outputs:
- serve_gate: bfloat16 [128, 2048, 768], P('owner', None, 'rows')
- serve_up: bfloat16 [128, 2048, 768], P('owner', None, 'rows')
- scale_gate: float32 [128, 768], P('owner', 'rows')
- scale_up: float32 [128, 768], P('owner', 'rows')
- serve_router: bfloat16 [2048, 128], replicated
All inputs are finite; a program needn't handle non-finite values. Where the computation divides by a largest or mean magnitude, that divisor is 1e-20 or more.
Results may differ from a plain program's by a relative error of at most 0.001.
Values may be sent and summed in bfloat16 or wider, within the bound.
No kernel may reach another device: no remote copies, remote signals or barrier semaphores. Data moves between devices by JAX's collectives and lax.ppermute only.
A program may use at most 192 MiB of HBM per device.

v0:
```python
import jax
import jax.numpy as jnp
from jax import lax
from jax.sharding import PartitionSpec as P

D_MODEL = 2048


def on_device(w_gate, w_up, router_weight, router_gain):
    total_gate, total_up = lax.psum(
        (jnp.sum(jnp.abs(w_gate), axis=1), jnp.sum(jnp.abs(w_up), axis=1)), "rows"
    )
    scale_gate = total_gate / D_MODEL
    scale_up = total_up / D_MODEL
    narrow_gate, narrow_up = (
        (w_gate / jnp.expand_dims(scale_gate, 1)).astype(jnp.bfloat16),
        (w_up / jnp.expand_dims(scale_up, 1)).astype(jnp.bfloat16),
    )
    serve_gate, serve_up = (
        lax.all_to_all(narrow_gate, "rows", split_axis=2, concat_axis=1, tiled=True),
        lax.all_to_all(narrow_up, "rows", split_axis=2, concat_axis=1, tiled=True),
    )
    scale_gate = lax.dynamic_slice_in_dim(
        scale_gate, lax.axis_index("rows") * serve_gate.shape[2], serve_gate.shape[2], axis=1
    )
    scale_up = lax.dynamic_slice_in_dim(
        scale_up, lax.axis_index("rows") * serve_up.shape[2], serve_up.shape[2], axis=1
    )
    part_router = (router_weight * router_gain[:, None]).astype(jnp.bfloat16)
    row_router = lax.all_gather(part_router, "rows", axis=0, tiled=True)
    serve_router = lax.all_gather(row_router, "owner", axis=1, tiled=True)
    return (serve_gate, serve_up, scale_gate, scale_up, serve_router)


def solution(mesh):
    placed = (P("owner", "rows", None), P("owner", "rows", None), P("rows", "owner"), P("rows"))
    return jax.shard_map(
        on_device,
        mesh=mesh,
        in_specs=placed,
        out_specs=(
            P("owner", None, "rows"),
            P("owner", None, "rows"),
            P("owner", "rows"),
            P("owner", "rows"),
            P(),
        ),
        check_vma=False,
    )
```

profile of v0, /device:TPU:0, one launch (start us, length us, event | category | flops | bytes accessed | tf_op | source)
XLA Modules:
  0.0 481.1 jit_solution(11326135817132377053)
XLA Ops:
  7.2 0.0 all-reduce.3.cloned.1.call-start
  7.2 17.4 %abs_reduce_fusion = (f32[32,768]{1,0:T(8,128)}, f32[32,768]{1,0:T(8,128)}) fusion(f32[32,256,768]{2,1,0:T(8,128)} %param.5, f32[32,256,768]{2,1,0:T(8,128)} %param.4), kind=kLoop, calls=%fused_computation.1 | loop fusion | flops 25116672 | bytes 50528256 | tf_op jit(solution)/shard_map/reduce_sum | solution.py:11
  24.6 0.0 all-reduce.3.cloned.1.call-update
  24.7 25.1 %copy.25 = f32[32,256,768]{1,0,2:T(8,128)} copy(f32[32,256,768]{2,1,0:T(8,128)} %param.5) | data formatting | bytes 50331648 | tf_op args[1]
  49.8 31.5 %all-reduce.3.cloned.1.call-done = (f32[32,768]{1,0:T(8,128)}, f32[32,768]{1,0:T(8,128)}) async-done(((f32[32,768]{1,0:T(8,128)}, f32[32,768]{1,0:T(8,128)}), (f32[32,768]{1,0:T(8,128)}, f32[32,768]{1,0:T(8,128)})) %all-reduce.3.cloned.1.call-update) | async-done | bytes 196624 | tf_op jit(solution)/shard_map/psum | solution.py:10
  81.3 0.9 broadcast_multiply_fusion
  82.2 0.2 copy.24
  82.4 14.1 %divide_convert_fusion = bf16[32,256,768]{1,0,2:T(8,128)(2,1)} fusion(f32[32,256,768]{1,0,2:T(8,128)} %copy.25, f32[32,768]{0,1:T(8,128)S(1)} %copy.24), kind=kLoop, calls=%fused_computation | loop fusion | flops 12582912 | bytes 37847040 | tf_op jit(solution)/shard_map/convert_element_type | solution.py:17
  96.5 5.4 %all-to-all-start.1 = ((bf16[32,256,768]{1,0,2:T(8,128)(2,1)}), bf16[32,256,768]{1,0,2:T(8,128)(2,1)}, u32[]{:S(2)}, u32[]{:S(2)}) async-start(bf16[32,256,768]{1,0,2:T(8,128)(2,1)} %divide_convert_fusion), calls=%async_computation.1 | async-start | bytes 25165824 | tf_op jit(solution)/shard_map/all_to_all | solution.py:21
  101.9 0.0 copy-start
  101.9 25.1 %copy.21 = f32[32,256,768]{1,0,2:T(8,128)} copy(f32[32,256,768]{2,1,0:T(8,128)} %param.4) | data formatting | bytes 50331648 | tf_op args[0]
  127.1 0.0 copy-done
  127.1 0.2 copy.20
  127.2 0.0 copy-start.1
  127.3 0.0 copy-start.2
  127.3 14.1 %divide_convert_fusion.1 = bf16[32,256,768]{1,0,2:T(8,128)(2,1)} fusion(f32[32,256,768]{1,0,2:T(8,128)} %copy.21, f32[32,768]{0,1:T(8,128)S(1)} %copy.20), kind=kLoop, calls=%fused_computation.2 | loop fusion | flops 12582912 | bytes 37847040 | tf_op jit(solution)/shard_map/convert_element_type | solution.py:16
  141.4 99.5 %all-to-all-done.1 = bf16[32,256,768]{1,0,2:T(8,128)(2,1)} async-done(((bf16[32,256,768]{1,0,2:T(8,128)(2,1)}), bf16[32,256,768]{1,0,2:T(8,128)(2,1)}, u32[]{:S(2)}, u32[]{:S(2)}) %all-to-all-start.1) | async-done | bytes 12582944 | tf_op jit(solution)/shard_map/all_to_all | solution.py:21
  240.9 5.4 %all-to-all-start = ((bf16[32,256,768]{1,0,2:T(8,128)(2,1)}), bf16[32,256,768]{1,0,2:T(8,128)(2,1)}, u32[]{:S(2)}, u32[]{:S(2)}) async-start(bf16[32,256,768]{1,0,2:T(8,128)(2,1)} %divide_convert_fusion.1), calls=%async_computation | async-start | bytes 25165824 | tf_op jit(solution)/shard_map/all_to_all | solution.py:20
  246.3 0.0 copy-done.1
  246.3 0.0 copy-done.2
  246.3 142.4 %all_gather.6 = bf16[2048,32]{0,1:T(8,128)(2,1)S(1)} all-gather(bf16[256,32]{0,1:T(8,128)(2,1)S(1)} %multiply_convert_fusion), channel_id=1, replica_groups=mesh['owner'=4,'rows'=8] {'rows'}, dimensions={0}, use_global_device_ids=true | all-gather | bytes 147456 | tf_op jit(solution)/shard_map/all_gather | solution.py:30
  388.8 16.1 %all_gather.7 = bf16[2048,128]{0,1:T(8,128)(2,1)S(1)} all-gather(bf16[2048,32]{0,1:T(8,128)(2,1)S(1)} %all_gather.6), channel_id=1, replica_groups=mesh['owner'=4,'rows'=8] {'owner'}, dimensions={1}, use_global_device_ids=true | all-gather | bytes 655360 | tf_op jit(solution)/shard_map/all_gather | solution.py:31
  404.8 1.0 copy.28
  405.8 0.7 constant_dynamic-slice_fusion
  406.5 0.7 constant_dynamic-slice_fusion.1
  407.2 14.1 %copy.27 = bf16[32,8,256,96]{2,1,3,0:T(8,128)(2,1)} copy(bf16[32,8,256,96]{2,0,3,1:T(8,128)(2,1)} %bitcast.5) | data formatting | bytes 25165824 | tf_op jit(solution)/shard_map/all_to_all | solution.py:21
  421.2 19.5 %all_to_all.33 = bf16[32,2048,96]{1,2,0:T(8,128)(2,1)} reshape(bf16[32,8,256,96]{2,1,3,0:T(8,128)(2,1)} %copy.27) | data formatting | bytes 25165824 | tf_op jit(solution)/shard_map/all_to_all | solution.py:21
  440.7 0.0 all-to-all-done
  440.7 14.1 %copy.23 = bf16[32,8,256,96]{2,1,3,0:T(8,128)(2,1)} copy(bf16[32,8,256,96]{2,0,3,1:T(8,128)(2,1)} %bitcast.2) | data formatting | bytes 25165824 | tf_op jit(solution)/shard_map/all_to_all | solution.py:20
  454.8 19.5 %all_to_all.29 = bf16[32,2048,96]{1,2,0:T(8,128)(2,1)} reshape(bf16[32,8,256,96]{2,1,3,0:T(8,128)(2,1)} %copy.23) | data formatting | bytes 25165824 | tf_op jit(solution)/shard_map/all_to_all | solution.py:20
  (2 shorter events, 0.0 us)
Async XLA Ops:
  7.2 74.2 %all-reduce.3.cloned.1.call-start = ((), (), s32[]{:S(2)}) async-start(), calls=%async_computation.2 | async-start | bytes 393216 | tf_op jit(solution)/shard_map/psum | solution.py:10
  96.5 144.4 %all-to-all-start.1 = ((bf16[32,256,768]{1,0,2:T(8,128)(2,1)}), bf16[32,256,768]{1,0,2:T(8,128)(2,1)}, u32[]{:S(2)}, u32[]{:S(2)}) async-start(bf16[32,256,768]{1,0,2:T(8,128)(2,1)} %divide_convert_fusion), calls=%async_computation.1 | async-start | bytes 25165824 | tf_op jit(solution)/shard_map/all_to_all | solution.py:21
  101.9 25.1 %copy-start = (f32[32,768]{1,0:T(8,128)S(1)}, f32[32,768]{1,0:T(8,128)}, u32[]{:S(2)}) copy-start(f32[32,768]{1,0:T(8,128)} %get-tuple-element.10) | copy-start | bytes 294916
  127.2 119.0 %copy-start.1 = (f32[256,32]{0,1:T(8,128)S(1)}, f32[256,32]{0,1:T(8,128)}, u32[]{:S(2)}) copy-start(f32[256,32]{0,1:T(8,128)} %param.6) | copy-start | bytes 98308
  127.3 119.0 %copy-start.2 = (f32[256]{0:T(256)S(1)}, f32[256]{0:T(256)}, u32[]{:S(2)}) copy-start(f32[256]{0:T(256)} %param.7) | copy-start | bytes 3076
  240.9 199.8 %all-to-all-start = ((bf16[32,256,768]{1,0,2:T(8,128)(2,1)}), bf16[32,256,768]{1,0,2:T(8,128)(2,1)}, u32[]{:S(2)}, u32[]{:S(2)}) async-start(bf16[32,256,768]{1,0,2:T(8,128)(2,1)} %divide_convert_fusion.1), calls=%async_computation | async-start | bytes 25165824 | tf_op jit(solution)/shard_map/all_to_all | solution.py:20
Sparse Core Ops, SparseCore 0:
  24.8 56.4 all-reduce.2
where the time goes:
time: 483 us; the launch traced here: 481 us
  blocking collectives  158 us (33%)
  waiting for transfers between devices  131 us (27%)
  local copies, waits for them, and re-layouts  120 us (25%)
  other arithmetic  46.6 us (10%)
  between operations  14.1 us (3%)
  starting transfers between devices  10.8 us (2%)
    all_gather x1, blocking collectives, on_device(): row_router = lax.all_gather(part_router, 'rows', axis=0, tiled=True)  142 us
    all_to_all x1, waiting for transfers between devices, on_device(): lax.all_to_all(narrow_up, 'rows', split_axis=2, concat_axis=1, tiled=True)  99.5 us
    unnamed x9, local copies, waits for them, and re-layouts  51.3 us
    all_to_all x2, local copies, waits for them, and re-layouts, on_device(): lax.all_to_all(narrow_gate, 'rows', split_axis=2, concat_axis=1, tiled=True)  33.6 us
    all_to_all x2, local copies, waits for them, and re-layouts, on_device(): lax.all_to_all(narrow_up, 'rows', split_axis=2, concat_axis=1, tiled=True)  33.6 us
    psum x1, waiting for transfers between devices, on_device(): lax.psum((jnp.sum(jnp.abs(w_gate), axis=1), jnp.sum(jnp.abs(w_up), axis=1...  31.5 us
    reduce_sum x1, other arithmetic, on_device(): jnp.sum(jnp.abs(w_up), axis=1)  17.4 us
    all_gather x1, blocking collectives, on_device(): serve_router = lax.all_gather(row_router, 'owner', axis=1, tiled=True)  16.1 us
  transfers between devices with their start and end apart: 3, of which 2 were waited for; matrix products, arithmetic and copies ran while one was open for 17% of the time, Pallas kernels for 0%

commit v1 on v0

v1 whole, which is shorter than its diff:
```python
import functools

import jax
import jax.numpy as jnp
from jax import lax
from jax.experimental import pallas as pl
from jax.experimental.pallas import tpu as pltpu
from jax.sharding import PartitionSpec as P


CHUNKS = (2, 4, 6, 6, 6, 4, 2, 1, 1)
ROUTER_CHUNK = 1
SPAN, BASE = 251.0, 125.0
SIDE = 8
LANES = 128


def pack_kernel(parts, count, routed, me, wg, wu, *rest):
    rw, gain, rest = (rest[0], rest[1], rest[2:]) if routed else (None, None, rest)
    outs, after, turned, tops = rest[:parts], rest[parts], rest[parts + 1], rest[parts + 2]
    after[0] = me[0]
    height = turned.shape[0] // parts
    e = pl.program_id(0)
    starts = [pl.multiple_of((me[0] ^ k) * height, height) for k in range(parts)]

    @pl.when(e < count)
    def _():
        for t, w in enumerate((wg, wu)):
            x = w[0]
            mag = jnp.abs(x)
            top = jnp.max(mag, axis=0, keepdims=True)
            top = (top * 1.0079).astype(jnp.bfloat16).astype(jnp.float32)
            tops[t, pl.ds(e, 1), :] = top
            part = mag * jnp.where(top > 1e-30, 1.0 / top, 0.0)
            root = part * lax.rsqrt(jnp.maximum(part, 1e-30))
            code = jnp.exp2(root * SPAN - BASE)
            code = jnp.where(x < 0, -code, code)
            turned[...] = code.T.astype(jnp.bfloat16)
            for k in range(parts):
                outs[k][t * height : (t + 1) * height, :] = turned[pl.ds(starts[k], height), :]

    @pl.when(e == count)
    def _():
        cols = turned.shape[0]
        at = 0
        if routed:
            at = rw.shape[0]
            made = (rw[...] * gain[...]).astype(jnp.bfloat16)
        for k in range(parts):
            if routed:
                outs[k][:at, :] = made
            for t in range(2):
                row = pltpu.roll(tops[t], cols - starts[k], 1)[:, :LANES]
                outs[k][at : at + SIDE, t * LANES : (t + 1) * LANES] = row.astype(jnp.bfloat16)


def pack(w_gate, w_up, routing, me, first, count, parts):
    _, rows, cols = w_gate.shape
    height = cols // parts
    last = count - 1
    block = pl.BlockSpec((1, rows, cols), lambda e, me: (first + jnp.minimum(e, last), 0, 0))
    whole = [pl.BlockSpec(r.shape, lambda e, me: (0, 0)) for r in routing]
    piece = pl.BlockSpec((2 * height, rows), lambda e, me: (e, 0))
    length = 2 * height * count + SIDE + (routing[0].shape[0] if routing else 0)
    return pl.pallas_call(
        functools.partial(pack_kernel, parts, count, bool(routing)),
        grid_spec=pltpu.PrefetchScalarGridSpec(
            num_scalar_prefetch=1,
            grid=(count + 1,),
            in_specs=[block, block] + whole,
            out_specs=[piece] * parts + [pl.BlockSpec(memory_space=pltpu.SMEM)],
            scratch_shapes=[
                pltpu.VMEM((cols, rows), jnp.bfloat16),
                pltpu.VMEM((2, SIDE, cols), jnp.float32),
            ],
        ),
        out_shape=[jax.ShapeDtypeStruct((length, rows), jnp.bfloat16)] * parts
        + [jax.ShapeDtypeStruct((1,), jnp.int32)],
        name="pack",
    )(me, w_gate, w_up, *routing)


def unpack_kernel(parts, first, routed, held, d_model, me, *refs):
    bulk, side, refs = refs[:parts], refs[parts : 2 * parts], refs[2 * parts :]
    if routed:
        routes, refs = refs[:parts], refs[parts:]
    if held:
        scales_in, refs = refs[2:4], refs[4:]
    outs, scales, refs = refs[:2], refs[2:4], refs[4:]
    tops = refs[-1]
    e = pl.program_id(0)
    height, rows = bulk[0].shape[0] // 2, bulk[0].shape[1]
    starts = [pl.multiple_of((me[0] ^ k) * rows, rows) for k in range(parts)]

    @pl.when(e == 0)
    def _():
        for t in range(2):
            if held:
                scales[t][...] = scales_in[t][...]
            for k in range(parts):
                tops[t, k * SIDE : (k + 1) * SIDE, :] = side[k][
                    :, t * LANES : (t + 1) * LANES
                ].astype(jnp.float32)
        if routed:
            for k in range(parts):
                refs[0][:, pl.ds(starts[k], rows)] = routes[k][...]

    step = 16
    down = lax.broadcasted_iota(jnp.int32, (step, LANES), 0)
    across = lax.broadcasted_iota(jnp.int32, (step, LANES), 1)
    for t in range(2):
        top = jnp.concatenate([tops[t, pl.ds(k * SIDE + e, 1), :] for k in range(parts)], axis=0)
        top = (top * (1.0 / (SPAN * SPAN))).T
        scale = jnp.zeros((1, LANES), jnp.float32)
        for r in range(0, height, step):
            values, total = [], jnp.zeros((step, rows), jnp.float32)
            for k in range(parts):
                code = bulk[k][t * height + r : t * height + r + step, :].astype(jnp.float32)
                root = jnp.log2(jnp.abs(code)) + BASE
                mag = root * root * top[r : r + step, k : k + 1]
                total = total + mag
                values.append(jnp.where(code < 0, -mag, mag))
            mean = jnp.sum(total, axis=1, keepdims=True) / d_model
            inverse = 1.0 / mean
            for k in range(parts):
                outs[t][0, r : r + step, pl.ds(starts[k], rows)] = (values[k] * inverse).astype(
                    jnp.bfloat16
                )
            scale = scale + jnp.sum(
                jnp.where(down + r == across, mean, 0.0), axis=0, keepdims=True
            )
        scales[t][pl.ds(first + e, 1), :] = scale[:, :height]


def unpack(pieces, held, me, first, count, experts, d_model, routes):
    parts = len(pieces)
    rows = pieces[0].shape[1]
    above = 2 * count * (pieces[0].shape[0] - SIDE - routes) // (2 * count)
    height = above // (2 * count)
    bulk = pl.BlockSpec((2 * height, rows), lambda e, me: (e, 0))
    side = pl.BlockSpec((SIDE, rows), lambda e, me: ((above + routes) // SIDE, 0))
    specs, operands = [bulk] * parts + [side] * parts, list(pieces) * 2
    if routes:
        specs += [pl.BlockSpec((routes, rows), lambda e, me: (above // routes, 0))] * parts
        operands += list(pieces)
    whole = pl.BlockSpec((experts, height), lambda e, me: (0, 0))
    aliases = {}
    if held is not None:
        aliases = {1 + len(operands) + i: i for i in range(4)}
        specs += [pl.BlockSpec(memory_space=pl.ANY)] * 2 + [whole] * 2
        operands += list(held)
    out = pl.BlockSpec((1, height, parts * rows), lambda e, me: (first + e, 0, 0))
    served = jax.ShapeDtypeStruct((experts, height, parts * rows), jnp.bfloat16)
    scale = jax.ShapeDtypeStruct((experts, height), jnp.float32)
    out_specs, out_shape = [out, out, whole, whole], [served, served, scale, scale]
    if routes:
        out_specs.append(pl.BlockSpec((routes, parts * rows), lambda e, me: (0, 0)))
        out_shape.append(jax.ShapeDtypeStruct((routes, parts * rows), jnp.bfloat16))
    return pl.pallas_call(
        functools.partial(unpack_kernel, parts, first, bool(routes), held is not None, d_model),
        grid_spec=pltpu.PrefetchScalarGridSpec(
            num_scalar_prefetch=1,
            grid=(count,),
            in_specs=specs,
            out_specs=out_specs,
            scratch_shapes=[pltpu.VMEM((2, parts * SIDE, LANES), jnp.float32)],
        ),
        out_shape=out_shape,
        input_output_aliases=aliases,
        name="unpack",
    )(me, *operands)


def exchanged(parts, d_model, w_gate, w_up, router_weight, router_gain):
    experts, rows, _ = w_gate.shape
    me = lax.axis_index("rows").astype(jnp.int32).reshape(1)
    arrived, first, turn = [], 0, me
    for c, count in enumerate(CHUNKS):
        routing = (router_weight.T, router_gain.reshape(1, rows)) if c == ROUTER_CHUNK else ()
        *pieces, turn = pack(w_gate, w_up, routing, turn, first, count, parts)
        moved = [pieces[0]]
        for k in range(1, parts):
            pairs = [(r, r ^ k) for r in range(parts)]
            moved.append(lax.ppermute(pieces[k], "rows", pairs))
        arrived.append((moved, first, count))
        first += count
    held = None
    for c, (moved, at, count) in enumerate(arrived):
        routes = router_weight.shape[1] if c == ROUTER_CHUNK else 0
        held = unpack(moved, held, me, at, count, experts, d_model, routes)
        if routes:
            *held, part = held
            whole = lax.all_gather(part, "owner", axis=0, tiled=True).T
            *held, serve_router = lax.optimization_barrier((*held, whole))
    gate, up, scale_gate, scale_up = held
    return jnp.swapaxes(gate, 1, 2), jnp.swapaxes(up, 1, 2), scale_gate, scale_up, serve_router


def plain(parts, d_model, w_gate, w_up, router_weight, router_gain):
    totals = lax.psum(tuple(jnp.sum(jnp.abs(w), axis=1) for w in (w_gate, w_up)), "rows")
    served, scales = [], []
    for w, total in zip((w_gate, w_up), totals):
        scale = total / d_model
        narrow = (w / jnp.expand_dims(scale, 1)).astype(jnp.bfloat16)
        served.append(lax.all_to_all(narrow, "rows", split_axis=2, concat_axis=1, tiled=True))
        width = scale.shape[1] // parts
        at = lax.axis_index("rows") * width
        scales.append(lax.dynamic_slice_in_dim(scale, at, width, axis=1))
    part = (router_weight * router_gain[:, None]).astype(jnp.bfloat16)
    part = lax.all_gather(part, "rows", axis=0, tiled=True)
    return (*served, *scales, lax.all_gather(part, "owner", axis=1, tiled=True))


def solution(mesh):
    parts = mesh.shape["rows"]

    def on_device(w_gate, w_up, router_weight, router_gain):
        experts, rows, cols = w_gate.shape
        fits = (
            parts & (parts - 1) == 0
            and rows == 2 * LANES
            and cols % (16 * parts) == 0
            and cols // parts <= LANES
            and router_weight.shape[1] % 16 == 0
            and (2 * cols // parts) % router_weight.shape[1] == 0
            and experts == sum(CHUNKS)
        )
        body = exchanged if fits else plain
        return body(parts, rows * parts, w_gate, w_up, router_weight, router_gain)

    return jax.shard_map(
        on_device,
        mesh=mesh,
        in_specs=(
            P("owner", "rows", None),
            P("owner", "rows", None),
            P("rows", "owner"),
            P("rows"),
        ),
        out_specs=(
            P("owner", None, "rows"),
            P("owner", None, "rows"),
            P("owner", "rows"),
            P("owner", "rows"),
            P(),
        ),
        check_vma=False,
    )
```

time: 483 us -> 459 us (0.950)
  blocking collectives: 158 us -> 16.8 us
  Pallas kernels: 0 us -> 140 us
  local copies, waits for them, and re-layouts: 120 us -> 7.26 us
  waiting for transfers between devices: 131 us -> 224 us
  starting transfers between devices: 10.8 us -> 68.7 us
  other arithmetic: 46.6 us -> 0 us
  between operations: 14.1 us -> 1.08 us
    ppermute x0 -> x63, waiting for transfers between devices: none -> 224 us  [exchanged(): moved.append(lax.ppermute(pieces[k], 'rows', pairs))]
    all_gather x2 -> x1, blocking collectives: 158 us -> 16.8 us  [exchanged(): whole = lax.all_gather(part, 'owner', axis=0, tiled=True).T]
    pallas_call x0 -> x18, Pallas kernels: none -> 140 us  [the longest x9 76 us: unpack(): pl.pallas_call(functools.partial(unpack_kernel, parts, first, bool(routes...]
    all_to_all x2 -> x0, waiting for transfers between devices: 99.5 us -> none  [the longest x1 99.5 us: on_device(): lax.all_to_all(narrow_up, 'rows', split_axis=2, concat_axis=1, tiled=True)]
    ppermute x0 -> x63, starting transfers between devices: none -> 68.7 us  [exchanged(): moved.append(lax.ppermute(pieces[k], 'rows', pairs))]
    all_to_all x4 -> x0, local copies, waits for them, and re-layouts: 67.1 us -> none  [the longest x2 33.6 us: on_device(): lax.all_to_all(narrow_gate, 'rows', split_axis=2, concat_axis=1, tiled=True)]
    unnamed x9 -> x97, local copies, waits for them, and re-layouts: 51.3 us -> 7.26 us
    psum x1 -> x0, waiting for transfers between devices: 31.5 us -> none  [on_device(): lax.psum((jnp.sum(jnp.abs(w_gate), axis=1), jnp.sum(jnp.abs(w_up), axis=1...]
  transfers between devices with their start and end apart: 3 -> 63, of which waited for: 2 -> 24; matrix products, arithmetic and copies ran while one was open for 17% -> 0% of each run, Pallas kernels for 0% -> 17%
where the time goes in v1:
time: 459 us; the launch traced here: 458 us
  waiting for transfers between devices  224 us (49%)
  Pallas kernels  140 us (31%)
  starting transfers between devices  68.7 us (15%)
  blocking collectives  16.8 us (4%)
  local copies, waits for them, and re-layouts  7.26 us (2%)
    ppermute x63, waiting for transfers between devices, exchanged(): moved.append(lax.ppermute(pieces[k], 'rows', pairs))  224 us
    pallas_call x9, Pallas kernels, unpack(): pl.pallas_call(functools.partial(unpack_kernel, parts, first, bool(routes...  76 us
    ppermute x63, starting transfers between devices, exchanged(): moved.append(lax.ppermute(pieces[k], 'rows', pairs))  68.7 us
    pallas_call x9, Pallas kernels, pack(): pl.pallas_call(functools.partial(pack_kernel, parts, count, bool(routing)...  63.6 us
    all_gather x1, blocking collectives, exchanged(): whole = lax.all_gather(part, 'owner', axis=0, tiled=True).T  16.8 us
  transfers between devices with their start and end apart: 63, of which 24 were waited for; matrix products, arithmetic and copies ran while one was open for 0% of the time, Pallas kernels for 17%

profile of v1, /device:TPU:0, one launch (start us, length us, event | category | flops | bytes accessed | tf_op | source)
XLA Modules:
  0.0 457.6 jit_solution(13210242789978719881)
XLA Ops:
  0.6 4.3 pack.9
  4.9 7.7 %pack.10 = (bf16[808,256]{1,0:T(8,128)(2,1)}, bf16[808,256]{1,0:T(8,128)(2,1)}, bf16[808,256]{1,0:T(8,128)(2,1)}, bf16[808,256]{1,0:T(8,128)(2,1)}, bf16[808,256...) custom-call(s32[1]{0:T(128)} %get-tuple-element.127.me, ...), custom_call_target="tpu_custom_call" | custom-call | tf_op jit(solution)/shard_map/pack/pallas_call | solution.py:65
  12.6 10.3 %pack.11 = (bf16[1160,256]{1,0:T(8,128)(2,1)}, bf16[1160,256]{1,0:T(8,128)(2,1)}, bf16[1160,256]{1,0:T(8,128)(2,1)}, bf16[1160,256]{1,0:T(8,128)(2,1)}, bf16[116...) custom-call(s32[1]{0:T(128)} %get-tuple-element.128.me, ...), custom_call_target="tpu_custom_call" | custom-call | tf_op jit(solution)/shard_map/pack/pallas_call | solution.py:65
  22.9 10.3 %pack.12 = (bf16[1160,256]{1,0:T(8,128)(2,1)}, bf16[1160,256]{1,0:T(8,128)(2,1)}, bf16[1160,256]{1,0:T(8,128)(2,1)}, bf16[1160,256]{1,0:T(8,128)(2,1)}, bf16[116...) custom-call(s32[1]{0:T(128)} %get-tuple-element.129.me, ...), custom_call_target="tpu_custom_call" | custom-call | tf_op jit(solution)/shard_map/pack/pallas_call | solution.py:65
  33.2 10.3 %pack.13 = (bf16[1160,256]{1,0:T(8,128)(2,1)}, bf16[1160,256]{1,0:T(8,128)(2,1)}, bf16[1160,256]{1,0:T(8,128)(2,1)}, bf16[1160,256]{1,0:T(8,128)(2,1)}, bf16[116...) custom-call(s32[1]{0:T(128)} %get-tuple-element.130.me, ...), custom_call_target="tpu_custom_call" | custom-call | tf_op jit(solution)/shard_map/pack/pallas_call | solution.py:65
  43.5 7.6 %pack.14 = (bf16[776,256]{1,0:T(8,128)(2,1)}, bf16[776,256]{1,0:T(8,128)(2,1)}, bf16[776,256]{1,0:T(8,128)(2,1)}, bf16[776,256]{1,0:T(8,128)(2,1)}, bf16[776,256...) custom-call(s32[1]{0:T(128)} %get-tuple-element.131.me, ...), custom_call_target="tpu_custom_call" | custom-call | tf_op jit(solution)/shard_map/pack/pallas_call | solution.py:65
  51.2 4.9 %pack.15 = (bf16[392,256]{1,0:T(8,128)(2,1)}, bf16[392,256]{1,0:T(8,128)(2,1)}, bf16[392,256]{1,0:T(8,128)(2,1)}, bf16[392,256]{1,0:T(8,128)(2,1)}, bf16[392,256...) custom-call(s32[1]{0:T(128)} %get-tuple-element.132.me, ...), custom_call_target="tpu_custom_call" | custom-call | tf_op jit(solution)/shard_map/pack/pallas_call | solution.py:65
  56.1 3.9 pack.16
  68.2 4.7 %collective-permute-done.11.refs_5_.refs_13_ = bf16[200,256]{1,0:T(8,128)(2,1)} collective-permute-done((bf16[200,256]{1,0:T(8,128)(2,1)}, bf16[200,256]{1,0:T(8,128)(2,1)}, u32[]{:S(2)}, u32[]{:S(2)}) %collective-permute-start.11) | collective-permute-done | bytes 102432 | tf_op jit(solution)/shard_map/ppermute | solution.py:184
  74.3 4.2 pack.17
  93.7 7.3 %collective-permute-done.60.refs_5_.refs_13_ = bf16[392,256]{1,0:T(8,128)(2,1)S(1)} collective-permute-done((bf16[392,256]{1,0:T(8,128)(2,1)}, bf16[392,256]{1,0:T(8,128)(2,1)S(1)}, u32[]{:S(2)}, u32[]{:S(2)}) %collective-permute-start.60) | collective-permute-done | bytes 200736 | tf_op jit(solution)/shard_map/ppermute | solution.py:184
  110.7 9.6 %collective-permute-done.17.refs_4_.refs_12_ = bf16[392,256]{1,0:T(8,128)(2,1)S(1)} collective-permute-done((bf16[392,256]{1,0:T(8,128)(2,1)}, bf16[392,256]{1,0:T(8,128)(2,1)S(1)}, u32[]{:S(2)}, u32[]{:S(2)}) %collective-permute-start.17) | collective-permute-done | bytes 200736 | tf_op jit(solution)/shard_map/ppermute | solution.py:184
  132.0 4.6 collective-permute-done.23.refs_3_.refs_11_
  142.0 10.7 %collective-permute-done.25.refs_5_.refs_13_ = bf16[776,256]{1,0:T(8,128)(2,1)S(1)} collective-permute-done((bf16[776,256]{1,0:T(8,128)(2,1)}, bf16[776,256]{1,0:T(8,128)(2,1)S(1)}, u32[]{:S(2)}, u32[]{:S(2)}) %collective-permute-start.25) | collective-permute-done | bytes 397344 | tf_op jit(solution)/shard_map/ppermute | solution.py:184
  154.3 15.8 %collective-permute-done.27.refs_7_.refs_15_ = bf16[776,256]{1,0:T(8,128)(2,1)S(1)} collective-permute-done((bf16[776,256]{1,0:T(8,128)(2,1)S(1)}, bf16[776,256]{1,0:T(8,128)(2,1)S(1)}, u32[]{:S(2)}, u32[]{:S(2)}) %collective-permute-start.27) | collective-permute-done | bytes 397344 | tf_op jit(solution)/shard_map/ppermute | solution.py:184
  176.5 23.0 %collective-permute-done.52.refs_4_.refs_12_.refs_20_ = bf16[808,256]{1,0:T(8,128)(2,1)S(1)} collective-permute-done((bf16[808,256]{1,0:T(8,128)(2,1)}, bf16[808,256]{1,0:T(8,128)(2,1)S(1)}, u32[]{:S(2)}, u32[]{:S(2)}) %collective-permute-start.52) | collective-permute-done | bytes 413728 | tf_op jit(solution)/shard_map/ppermute | solution.py:184
  202.6 7.5 %collective-permute-done.53.refs_5_.refs_13_.refs_21_ = bf16[808,256]{1,0:T(8,128)(2,1)S(1)} collective-permute-done((bf16[808,256]{1,0:T(8,128)(2,1)}, bf16[808,256]{1,0:T(8,128)(2,1)S(1)}, u32[]{:S(2)}, u32[]{:S(2)}) %collective-permute-start.53) | collective-permute-done | bytes 413728 | tf_op jit(solution)/shard_map/ppermute | solution.py:184
  217.9 13.2 %collective-permute-done.44.refs_3_.refs_11_ = bf16[1160,256]{1,0:T(8,128)(2,1)} collective-permute-done((bf16[1160,256]{1,0:T(8,128)(2,1)}, bf16[1160,256]{1,0:T(8,128)(2,1)}, u32[]{:S(2)}, u32[]{:S(2)}) %collective-permute-start.44) | collective-permute-done | bytes 593952 | tf_op jit(solution)/shard_map/ppermute | solution.py:184
  232.0 33.5 %collective-permute-done.46.refs_5_.refs_13_ = bf16[1160,256]{1,0:T(8,128)(2,1)} collective-permute-done((bf16[1160,256]{1,0:T(8,128)(2,1)}, bf16[1160,256]{1,0:T(8,128)(2,1)}, u32[]{:S(2)}, u32[]{:S(2)}) %collective-permute-start.46) | collective-permute-done | bytes 593952 | tf_op jit(solution)/shard_map/ppermute | solution.py:184
  270.2 10.9 %collective-permute-done.37.refs_3_.refs_11_ = bf16[1160,256]{1,0:T(8,128)(2,1)} collective-permute-done((bf16[1160,256]{1,0:T(8,128)(2,1)}, bf16[1160,256]{1,0:T(8,128)(2,1)}, u32[]{:S(2)}, u32[]{:S(2)}) %collective-permute-start.37) | collective-permute-done | bytes 593952 | tf_op jit(solution)/shard_map/ppermute | solution.py:184
  282.3 25.6 %collective-permute-done.38.refs_4_.refs_12_ = bf16[1160,256]{1,0:T(8,128)(2,1)} collective-permute-done((bf16[1160,256]{1,0:T(8,128)(2,1)}, bf16[1160,256]{1,0:T(8,128)(2,1)}, u32[]{:S(2)}, u32[]{:S(2)}) %collective-permute-start.38) | collective-permute-done | bytes 593952 | tf_op jit(solution)/shard_map/ppermute | solution.py:184
  309.6 9.3 %collective-permute-done.39.refs_5_.refs_13_ = bf16[1160,256]{1,0:T(8,128)(2,1)} collective-permute-done((bf16[1160,256]{1,0:T(8,128)(2,1)}, bf16[1160,256]{1,0:T(8,128)(2,1)}, u32[]{:S(2)}, u32[]{:S(2)}) %collective-permute-start.39) | collective-permute-done | bytes 593952 | tf_op jit(solution)/shard_map/ppermute | solution.py:184
  325.4 5.5 %unpack.9 = (bf16[32,96,2048]{2,1,0:T(8,128)(2,1)}, bf16[32,96,2048]{2,1,0:T(8,128)(2,1)}, f32[32,96]{1,0:T(8,128)}, f32[32,96]{1,0:T(8,128)}) custom-call(s32[1]{0:T(128)} %bitcast.me, bf16[392,256]{1,0:T(8,128)(2,1)} %get-tuple-element.199.refs_0_.refs_8_, bf16[392,256]{1,0:T(8,128)(2,1)} %copy-done.22, bf16[392,256]{1,0:T(8,128)(2,1)} %copy-done.23, ...), custom_call_target="tpu_custom_call" | custom-call | tf_op jit(solution)/shard_map/unpack/pallas_call | solution.py:159
  330.9 9.4 %unpack.10 = (bf16[32,96,2048]{2,1,0:T(8,128)(2,1)}, bf16[32,96,2048]{2,1,0:T(8,128)(2,1)}, f32[32,96]{1,0:T(8,128)}, f32[32,96]{1,0:T(8,128)}, bf16[32,2048]{1,0:T(8,128)(2,1)}) custom-call(s32[1]{0:T(128)} %bitcast.me, ...), custom_call_target="tpu_custom_call", output_to_operand_aliasing={{0}: (25, {}), {1}: (26, {}), {2}: (27, {}), {3}: (28, {})} | custom-call | tf_op jit(solution)/shard_map/unpack/pallas_call | solution.py:159
  340.4 22.6 %collective-permute-done.31.refs_4_.refs_12_ = bf16[1160,256]{1,0:T(8,128)(2,1)} collective-permute-done((bf16[1160,256]{1,0:T(8,128)(2,1)}, bf16[1160,256]{1,0:T(8,128)(2,1)}, u32[]{:S(2)}, u32[]{:S(2)}) %collective-permute-start.31) | collective-permute-done | bytes 593952 | tf_op jit(solution)/shard_map/ppermute | solution.py:184
  363.3 10.2 %collective-permute-done.32.refs_5_.refs_13_ = bf16[1160,256]{1,0:T(8,128)(2,1)} collective-permute-done((bf16[1160,256]{1,0:T(8,128)(2,1)}, bf16[1160,256]{1,0:T(8,128)(2,1)}, u32[]{:S(2)}, u32[]{:S(2)}) %collective-permute-start.32) | collective-permute-done | bytes 593952 | tf_op jit(solution)/shard_map/ppermute | solution.py:184
  377.8 16.8 %all_gather.3 = bf16[128,2048]{1,0:T(8,128)(2,1)S(1)} all-gather(bf16[32,2048]{1,0:T(8,128)(2,1)} %get-tuple-element.215), channel_id=1, replica_groups=mesh['owner'=4,'rows'=8] {'owner'}, dimensions={0}, use_global_device_ids=true | all-gather | bytes 655360 | tf_op jit(solution)/shard_map/all_gather | solution.py:193
  395.7 13.1 %unpack.11 = (bf16[32,96,2048]{2,1,0:T(8,128)(2,1)}, bf16[32,96,2048]{2,1,0:T(8,128)(2,1)}, f32[32,96]{1,0:T(8,128)}, f32[32,96]{1,0:T(8,128)}) custom-call(s32[1]{0:T(128)} %bitcast.me, bf16[1160,256]{1,0:T(8,128)(2,1)} %get-tuple-element.183.refs_0_.refs_8_, ...), custom_call_target="tpu_custom_call", output_to_operand_aliasing={{0}: (17, {}), {1}: (18, {}), {2}: (19, {}), {3}: (20, {})} | custom-call | tf_op jit(solution)/shard_map/unpack/pallas_call | solution.py:159
  408.8 12.9 %unpack.12 = (bf16[32,96,2048]{2,1,0:T(8,128)(2,1)}, bf16[32,96,2048]{2,1,0:T(8,128)(2,1)}, f32[32,96]{1,0:T(8,128)}, f32[32,96]{1,0:T(8,128)}) custom-call(s32[1]{0:T(128)} %bitcast.me, bf16[1160,256]{1,0:T(8,128)(2,1)} %get-tuple-element.175.refs_0_.refs_8_, ...), custom_call_target="tpu_custom_call", output_to_operand_aliasing={{0}: (17, {}), {1}: (18, {}), {2}: (19, {}), {3}: (20, {})} | custom-call | tf_op jit(solution)/shard_map/unpack/pallas_call | solution.py:159
  421.7 12.9 %unpack.13 = (bf16[32,96,2048]{2,1,0:T(8,128)(2,1)}, bf16[32,96,2048]{2,1,0:T(8,128)(2,1)}, f32[32,96]{1,0:T(8,128)}, f32[32,96]{1,0:T(8,128)}) custom-call(s32[1]{0:T(128)} %bitcast.me, bf16[1160,256]{1,0:T(8,128)(2,1)} %get-tuple-element.167.refs_0_.refs_8_, ...), custom_call_target="tpu_custom_call", output_to_operand_aliasing={{0}: (17, {}), {1}: (18, {}), {2}: (19, {}), {3}: (20, {})} | custom-call | tf_op jit(solution)/shard_map/unpack/pallas_call | solution.py:159
  434.6 9.2 %unpack.14 = (bf16[32,96,2048]{2,1,0:T(8,128)(2,1)}, bf16[32,96,2048]{2,1,0:T(8,128)(2,1)}, f32[32,96]{1,0:T(8,128)}, f32[32,96]{1,0:T(8,128)}) custom-call(s32[1]{0:T(128)} %bitcast.me, bf16[776,256]{1,0:T(8,128)(2,1)} %get-tuple-element.159.refs_0_.refs_8_, ...), custom_call_target="tpu_custom_call", output_to_operand_aliasing={{0}: (17, {}), {1}: (18, {}), {2}: (19, {}), {3}: (20, {})} | custom-call | tf_op jit(solution)/shard_map/unpack/pallas_call | solution.py:159
  443.8 5.5 %unpack.15 = (bf16[32,96,2048]{2,1,0:T(8,128)(2,1)}, bf16[32,96,2048]{2,1,0:T(8,128)(2,1)}, f32[32,96]{1,0:T(8,128)}, f32[32,96]{1,0:T(8,128)}) custom-call(s32[1]{0:T(128)} %bitcast.me, bf16[392,256]{1,0:T(8,128)(2,1)} %get-tuple-element.151.refs_0_.refs_8_, ...), custom_call_target="tpu_custom_call", output_to_operand_aliasing={{0}: (17, {}), {1}: (18, {}), {2}: (19, {}), {3}: (20, {})} | custom-call | tf_op jit(solution)/shard_map/unpack/pallas_call | solution.py:159
  (210 shorter events, 99.1 us)
Async XLA Ops:
  126.7 25.9 %collective-permute-start.25 = (bf16[776,256]{1,0:T(8,128)(2,1)}, bf16[776,256]{1,0:T(8,128)(2,1)S(1)}, u32[]{:S(2)}, u32[]{:S(2)}) collective-permute-start(bf16[776,256]{1,0:T(8,128)(2,1)} %get-tuple-element.164), channel_id=1, source_target_pairs={{0,5},{1,4},{2,7},{3,6},{4,1},{5,0},{6,3},{7,2},{8,13},{9,12},{10,... | collective-permute-start | bytes 1191944 | tf_op jit(solution)/shard_map/ppermute | solution.py:184
  127.2 27.0 %collective-permute-start.26 = (bf16[776,256]{1,0:T(8,128)(2,1)S(1)}, bf16[776,256]{1,0:T(8,128)(2,1)S(1)}, u32[]{:S(2)}, u32[]{:S(2)}) collective-permute-start(bf16[776,256]{1,0:T(8,128)(2,1)S(1)} %copy-done.45), channel_id=1, source_target_pairs={{0,6},{1,7},{2,4},{3,5},{4,2},{5,3},{6,0},{7,1},{8,14},{9,15},{10,... | collective-permute-start | bytes 1191944 | tf_op jit(solution)/shard_map/ppermute | solution.py:184
  132.0 40.4 %collective-permute-start.49 = (bf16[808,256]{1,0:T(8,128)(2,1)S(1)}, bf16[808,256]{1,0:T(8,128)(2,1)S(1)}, u32[]{:S(2)}, u32[]{:S(2)}) collective-permute-start(bf16[808,256]{1,0:T(8,128)(2,1)S(1)} %copy-done.43), channel_id=1, source_target_pairs={{0,1},{1,0},{2,3},{3,2},{4,5},{5,4},{6,7},{7,6},{8,9},{9,8},{10,11... | collective-permute-start | bytes 1241096 | tf_op jit(solution)/shard_map/ppermute | solution.py:184
  136.6 38.3 %collective-permute-start.50 = (bf16[808,256]{1,0:T(8,128)(2,1)S(1)}, bf16[808,256]{1,0:T(8,128)(2,1)S(1)}, u32[]{:S(2)}, u32[]{:S(2)}) collective-permute-start(bf16[808,256]{1,0:T(8,128)(2,1)S(1)} %copy-done.42), channel_id=1, source_target_pairs={{0,2},{1,3},{2,0},{3,1},{4,6},{5,7},{6,4},{7,5},{8,10},{9,11},{10,... | collective-permute-start | bytes 1241096 | tf_op jit(solution)/shard_map/ppermute | solution.py:184
  140.1 35.1 %collective-permute-start.51 = (bf16[808,256]{1,0:T(8,128)(2,1)S(1)}, bf16[808,256]{1,0:T(8,128)(2,1)S(1)}, u32[]{:S(2)}, u32[]{:S(2)}) collective-permute-start(bf16[808,256]{1,0:T(8,128)(2,1)S(1)} %copy-done.41), channel_id=1, source_target_pairs={{0,3},{1,2},{2,1},{3,0},{4,7},{5,6},{6,5},{7,4},{8,11},{9,10},{10,... | collective-permute-start | bytes 1241096 | tf_op jit(solution)/shard_map/ppermute | solution.py:184
  154.3 59.1 %collective-permute-start.42 = (bf16[1160,256]{1,0:T(8,128)(2,1)}, bf16[1160,256]{1,0:T(8,128)(2,1)S(1)}, u32[]{:S(2)}, u32[]{:S(2)}) collective-permute-start(bf16[1160,256]{1,0:T(8,128)(2,1)} %get-tuple-element.184), channel_id=1, source_target_pairs={{0,1},{1,0},{2,3},{3,2},{4,5},{5,4},{6,7},{7,6},{8,9},{9,8},{10,11... | collective-permute-start | bytes 1781768 | tf_op jit(solution)/shard_map/ppermute | solution.py:184
  170.8 28.7 %collective-permute-start.52 = (bf16[808,256]{1,0:T(8,128)(2,1)}, bf16[808,256]{1,0:T(8,128)(2,1)S(1)}, u32[]{:S(2)}, u32[]{:S(2)}) collective-permute-start(bf16[808,256]{1,0:T(8,128)(2,1)} %get-tuple-element.195), channel_id=1, source_target_pairs={{0,4},{1,5},{2,6},{3,7},{4,0},{5,1},{6,2},{7,3},{8,12},{9,13},{10,... | collective-permute-start | bytes 1241096 | tf_op jit(solution)/shard_map/ppermute | solution.py:184
  172.3 37.8 %collective-permute-start.53 = (bf16[808,256]{1,0:T(8,128)(2,1)}, bf16[808,256]{1,0:T(8,128)(2,1)S(1)}, u32[]{:S(2)}, u32[]{:S(2)}) collective-permute-start(bf16[808,256]{1,0:T(8,128)(2,1)} %get-tuple-element.196), channel_id=1, source_target_pairs={{0,5},{1,4},{2,7},{3,6},{4,1},{5,0},{6,3},{7,2},{8,13},{9,12},{10,... | collective-permute-start | bytes 1241096 | tf_op jit(solution)/shard_map/ppermute | solution.py:184
  174.9 36.4 %collective-permute-start.54 = (bf16[808,256]{1,0:T(8,128)(2,1)}, bf16[808,256]{1,0:T(8,128)(2,1)S(1)}, u32[]{:S(2)}, u32[]{:S(2)}) collective-permute-start(bf16[808,256]{1,0:T(8,128)(2,1)} %get-tuple-element.197), channel_id=1, source_target_pairs={{0,6},{1,7},{2,4},{3,5},{4,2},{5,3},{6,0},{7,1},{8,14},{9,15},{10,... | collective-permute-start | bytes 1241096 | tf_op jit(solution)/shard_map/ppermute | solution.py:184
  175.2 37.3 %collective-permute-start.55 = (bf16[808,256]{1,0:T(8,128)(2,1)}, bf16[808,256]{1,0:T(8,128)(2,1)S(1)}, u32[]{:S(2)}, u32[]{:S(2)}) collective-permute-start(bf16[808,256]{1,0:T(8,128)(2,1)} %get-tuple-element.198), channel_id=1, source_target_pairs={{0,7},{1,6},{2,5},{3,4},{4,3},{5,2},{6,1},{7,0},{8,15},{9,14},{10,... | collective-permute-start | bytes 1241096 | tf_op jit(solution)/shard_map/ppermute | solution.py:184
  210.1 21.0 %collective-permute-start.44 = (bf16[1160,256]{1,0:T(8,128)(2,1)}, bf16[1160,256]{1,0:T(8,128)(2,1)}, u32[]{:S(2)}, u32[]{:S(2)}) collective-permute-start(bf16[1160,256]{1,0:T(8,128)(2,1)} %get-tuple-element.186), channel_id=1, source_target_pairs={{0,3},{1,2},{2,1},{3,0},{4,7},{5,6},{6,5},{7,4},{8,11},{9,10},{10,... | collective-permute-start | bytes 1781768 | tf_op jit(solution)/shard_map/ppermute | solution.py:184
  211.3 19.8 %collective-permute-start.45 = (bf16[1160,256]{1,0:T(8,128)(2,1)}, bf16[1160,256]{1,0:T(8,128)(2,1)}, u32[]{:S(2)}, u32[]{:S(2)}) collective-permute-start(bf16[1160,256]{1,0:T(8,128)(2,1)} %get-tuple-element.187), channel_id=1, source_target_pairs={{0,4},{1,5},{2,6},{3,7},{4,0},{5,1},{6,2},{7,3},{8,12},{9,13},{10,... | collective-permute-start | bytes 1781768 | tf_op jit(solution)/shard_map/ppermute | solution.py:184
  212.5 53.1 %collective-permute-start.46 = (bf16[1160,256]{1,0:T(8,128)(2,1)}, bf16[1160,256]{1,0:T(8,128)(2,1)}, u32[]{:S(2)}, u32[]{:S(2)}) collective-permute-start(bf16[1160,256]{1,0:T(8,128)(2,1)} %get-tuple-element.188), channel_id=1, source_target_pairs={{0,5},{1,4},{2,7},{3,6},{4,1},{5,0},{6,3},{7,2},{8,13},{9,12},{10,... | collective-permute-start | bytes 1781768 | tf_op jit(solution)/shard_map/ppermute | solution.py:184
  213.4 52.4 %collective-permute-start.47 = (bf16[1160,256]{1,0:T(8,128)(2,1)}, bf16[1160,256]{1,0:T(8,128)(2,1)}, u32[]{:S(2)}, u32[]{:S(2)}) collective-permute-start(bf16[1160,256]{1,0:T(8,128)(2,1)} %get-tuple-element.189), channel_id=1, source_target_pairs={{0,6},{1,7},{2,4},{3,5},{4,2},{5,3},{6,0},{7,1},{8,14},{9,15},{10,... | collective-permute-start | bytes 1781768 | tf_op jit(solution)/shard_map/ppermute | solution.py:184
  216.7 49.8 %collective-permute-start.48 = (bf16[1160,256]{1,0:T(8,128)(2,1)}, bf16[1160,256]{1,0:T(8,128)(2,1)}, u32[]{:S(2)}, u32[]{:S(2)}) collective-permute-start(bf16[1160,256]{1,0:T(8,128)(2,1)} %get-tuple-element.190), channel_id=1, source_target_pairs={{0,7},{1,6},{2,5},{3,4},{4,3},{5,2},{6,1},{7,0},{8,15},{9,14},{10,... | collective-permute-start | bytes 1781768 | tf_op jit(solution)/shard_map/ppermute | solution.py:184
  231.1 36.2 %collective-permute-start.35 = (bf16[1160,256]{1,0:T(8,128)(2,1)}, bf16[1160,256]{1,0:T(8,128)(2,1)}, u32[]{:S(2)}, u32[]{:S(2)}) collective-permute-start(bf16[1160,256]{1,0:T(8,128)(2,1)} %get-tuple-element.176), channel_id=1, source_target_pairs={{0,1},{1,0},{2,3},{3,2},{4,5},{5,4},{6,7},{7,6},{8,9},{9,8},{10,11... | collective-permute-start | bytes 1781768 | tf_op jit(solution)/shard_map/ppermute | solution.py:184
  231.1 38.0 %collective-permute-start.36 = (bf16[1160,256]{1,0:T(8,128)(2,1)}, bf16[1160,256]{1,0:T(8,128)(2,1)}, u32[]{:S(2)}, u32[]{:S(2)}) collective-permute-start(bf16[1160,256]{1,0:T(8,128)(2,1)} %get-tuple-element.177), channel_id=1, source_target_pairs={{0,2},{1,3},{2,0},{3,1},{4,6},{5,7},{6,4},{7,5},{8,10},{9,11},{10,... | collective-permute-start | bytes 1781768 | tf_op jit(solution)/shard_map/ppermute | solution.py:184
  265.8 42.1 %collective-permute-start.38 = (bf16[1160,256]{1,0:T(8,128)(2,1)}, bf16[1160,256]{1,0:T(8,128)(2,1)}, u32[]{:S(2)}, u32[]{:S(2)}) collective-permute-start(bf16[1160,256]{1,0:T(8,128)(2,1)} %get-tuple-element.179), channel_id=1, source_target_pairs={{0,4},{1,5},{2,6},{3,7},{4,0},{5,1},{6,2},{7,3},{8,12},{9,13},{10,... | collective-permute-start | bytes 1781768 | tf_op jit(solution)/shard_map/ppermute | solution.py:184
  266.5 52.5 %collective-permute-start.39 = (bf16[1160,256]{1,0:T(8,128)(2,1)}, bf16[1160,256]{1,0:T(8,128)(2,1)}, u32[]{:S(2)}, u32[]{:S(2)}) collective-permute-start(bf16[1160,256]{1,0:T(8,128)(2,1)} %get-tuple-element.180), channel_id=1, source_target_pairs={{0,5},{1,4},{2,7},{3,6},{4,1},{5,0},{6,3},{7,2},{8,13},{9,12},{10,... | collective-permute-start | bytes 1781768 | tf_op jit(solution)/shard_map/ppermute | solution.py:184
  267.3 53.7 %collective-permute-start.40 = (bf16[1160,256]{1,0:T(8,128)(2,1)}, bf16[1160,256]{1,0:T(8,128)(2,1)}, u32[]{:S(2)}, u32[]{:S(2)}) collective-permute-start(bf16[1160,256]{1,0:T(8,128)(2,1)} %get-tuple-element.181), channel_id=1, source_target_pairs={{0,6},{1,7},{2,4},{3,5},{4,2},{5,3},{6,0},{7,1},{8,14},{9,15},{10,... | collective-permute-start | bytes 1781768 | tf_op jit(solution)/shard_map/ppermute | solution.py:184
  269.1 52.1 %collective-permute-start.41 = (bf16[1160,256]{1,0:T(8,128)(2,1)}, bf16[1160,256]{1,0:T(8,128)(2,1)}, u32[]{:S(2)}, u32[]{:S(2)}) collective-permute-start(bf16[1160,256]{1,0:T(8,128)(2,1)} %get-tuple-element.182), channel_id=1, source_target_pairs={{0,7},{1,6},{2,5},{3,4},{4,3},{5,2},{6,1},{7,0},{8,15},{9,14},{10,... | collective-permute-start | bytes 1781768 | tf_op jit(solution)/shard_map/ppermute | solution.py:184
  281.1 41.1 %collective-permute-start.28 = (bf16[1160,256]{1,0:T(8,128)(2,1)}, bf16[1160,256]{1,0:T(8,128)(2,1)}, u32[]{:S(2)}, u32[]{:S(2)}) collective-permute-start(bf16[1160,256]{1,0:T(8,128)(2,1)} %get-tuple-element.168), channel_id=1, source_target_pairs={{0,1},{1,0},{2,3},{3,2},{4,5},{5,4},{6,7},{7,6},{8,9},{9,8},{10,11... | collective-permute-start | bytes 1781768 | tf_op jit(solution)/shard_map/ppermute | solution.py:184
  319.0 21.4 %collective-permute-start.30 = (bf16[1160,256]{1,0:T(8,128)(2,1)}, bf16[1160,256]{1,0:T(8,128)(2,1)}, u32[]{:S(2)}, u32[]{:S(2)}) collective-permute-start(bf16[1160,256]{1,0:T(8,128)(2,1)} %get-tuple-element.170), channel_id=1, source_target_pairs={{0,3},{1,2},{2,1},{3,0},{4,7},{5,6},{6,5},{7,4},{8,11},{9,10},{10,... | collective-permute-start | bytes 1781768 | tf_op jit(solution)/shard_map/ppermute | solution.py:184
  321.0 42.1 %collective-permute-start.31 = (bf16[1160,256]{1,0:T(8,128)(2,1)}, bf16[1160,256]{1,0:T(8,128)(2,1)}, u32[]{:S(2)}, u32[]{:S(2)}) collective-permute-start(bf16[1160,256]{1,0:T(8,128)(2,1)} %get-tuple-element.171), channel_id=1, source_target_pairs={{0,4},{1,5},{2,6},{3,7},{4,0},{5,1},{6,2},{7,3},{8,12},{9,13},{10,... | collective-permute-start | bytes 1781768 | tf_op jit(solution)/shard_map/ppermute | solution.py:184
  321.3 52.3 %collective-permute-start.32 = (bf16[1160,256]{1,0:T(8,128)(2,1)}, bf16[1160,256]{1,0:T(8,128)(2,1)}, u32[]{:S(2)}, u32[]{:S(2)}) collective-permute-start(bf16[1160,256]{1,0:T(8,128)(2,1)} %get-tuple-element.172), channel_id=1, source_target_pairs={{0,5},{1,4},{2,7},{3,6},{4,1},{5,0},{6,3},{7,2},{8,13},{9,12},{10,... | collective-permute-start | bytes 1781768 | tf_op jit(solution)/shard_map/ppermute | solution.py:184
  322.2 53.3 %collective-permute-start.33 = (bf16[1160,256]{1,0:T(8,128)(2,1)}, bf16[1160,256]{1,0:T(8,128)(2,1)}, u32[]{:S(2)}, u32[]{:S(2)}) collective-permute-start(bf16[1160,256]{1,0:T(8,128)(2,1)} %get-tuple-element.173), channel_id=1, source_target_pairs={{0,6},{1,7},{2,4},{3,5},{4,2},{5,3},{6,0},{7,1},{8,14},{9,15},{10,... | collective-permute-start | bytes 1781768 | tf_op jit(solution)/shard_map/ppermute | solution.py:184
  323.8 53.4 %collective-permute-start.34 = (bf16[1160,256]{1,0:T(8,128)(2,1)}, bf16[1160,256]{1,0:T(8,128)(2,1)}, u32[]{:S(2)}, u32[]{:S(2)}) collective-permute-start(bf16[1160,256]{1,0:T(8,128)(2,1)} %get-tuple-element.174), channel_id=1, source_target_pairs={{0,7},{1,6},{2,5},{3,4},{4,3},{5,2},{6,1},{7,0},{8,15},{9,14},{10,... | collective-permute-start | bytes 1781768 | tf_op jit(solution)/shard_map/ppermute | solution.py:184
  340.4 112.7 %collective-permute-start.2 = (bf16[200,256]{1,0:T(8,128)(2,1)}, bf16[200,256]{1,0:T(8,128)(2,1)S(1)}, u32[]{:S(2)}, u32[]{:S(2)}) collective-permute-start(bf16[200,256]{1,0:T(8,128)(2,1)} %get-tuple-element.138), channel_id=1, source_target_pairs={{0,3},{1,2},{2,1},{3,0},{4,7},{5,6},{6,5},{7,4},{8,11},{9,10},{10,... | collective-permute-start | bytes 307208 | tf_op jit(solution)/shard_map/ppermute | solution.py:184
  363.0 90.1 %collective-permute-start.3 = (bf16[200,256]{1,0:T(8,128)(2,1)}, bf16[200,256]{1,0:T(8,128)(2,1)S(1)}, u32[]{:S(2)}, u32[]{:S(2)}) collective-permute-start(bf16[200,256]{1,0:T(8,128)(2,1)} %get-tuple-element.139), channel_id=1, source_target_pairs={{0,4},{1,5},{2,6},{3,7},{4,0},{5,1},{6,2},{7,3},{8,12},{9,13},{10,... | collective-permute-start | bytes 307208 | tf_op jit(solution)/shard_map/ppermute | solution.py:184
  373.6 79.6 %collective-permute-start.4 = (bf16[200,256]{1,0:T(8,128)(2,1)}, bf16[200,256]{1,0:T(8,128)(2,1)S(1)}, u32[]{:S(2)}, u32[]{:S(2)}) collective-permute-start(bf16[200,256]{1,0:T(8,128)(2,1)} %get-tuple-element.140), channel_id=1, source_target_pairs={{0,5},{1,4},{2,7},{3,6},{4,1},{5,0},{6,3},{7,2},{8,13},{9,12},{10,... | collective-permute-start | bytes 307208 | tf_op jit(solution)/shard_map/ppermute | solution.py:184
  375.5 77.7 %collective-permute-start.5 = (bf16[200,256]{1,0:T(8,128)(2,1)}, bf16[200,256]{1,0:T(8,128)(2,1)S(1)}, u32[]{:S(2)}, u32[]{:S(2)}) collective-permute-start(bf16[200,256]{1,0:T(8,128)(2,1)} %get-tuple-element.141), channel_id=1, source_target_pairs={{0,6},{1,7},{2,4},{3,5},{4,2},{5,3},{6,0},{7,1},{8,14},{9,15},{10,... | collective-permute-start | bytes 307208 | tf_op jit(solution)/shard_map/ppermute | solution.py:184
  377.2 76.0 %collective-permute-start.6 = (bf16[200,256]{1,0:T(8,128)(2,1)}, bf16[200,256]{1,0:T(8,128)(2,1)S(1)}, u32[]{:S(2)}, u32[]{:S(2)}) collective-permute-start(bf16[200,256]{1,0:T(8,128)(2,1)} %get-tuple-element.142), channel_id=1, source_target_pairs={{0,7},{1,6},{2,5},{3,4},{4,3},{5,2},{6,1},{7,0},{8,15},{9,14},{10,... | collective-permute-start | bytes 307208 | tf_op jit(solution)/shard_map/ppermute | solution.py:184
  (79 other events, 2651.2 us)

commit v2 on v1

--- a/solution.py
+++ b/solution.py
@@ -8,16 +8,17 @@
 from jax.sharding import PartitionSpec as P
 
 
-CHUNKS = (2, 4, 6, 6, 6, 4, 2, 1, 1)
+CHUNKS = (2, 6, 8, 8, 5, 2, 1)
 ROUTER_CHUNK = 1
 SPAN, BASE = 251.0, 125.0
 SIDE = 8
+LN2 = 0.6931471805599453
 LANES = 128
 
 
 def pack_kernel(parts, count, routed, me, wg, wu, *rest):
     rw, gain, rest = (rest[0], rest[1], rest[2:]) if routed else (None, None, rest)
-    outs, after, turned, tops = rest[:parts], rest[parts], rest[parts + 1], rest[parts + 2]
+    outs, (after, turned, tops, sides) = rest[:parts], rest[parts:]
     after[0] = me[0]
     height = turned.shape[0] // parts
     e = pl.program_id(0)
@@ -31,27 +32,28 @@
             top = jnp.max(mag, axis=0, keepdims=True)
             top = (top * 1.0079).astype(jnp.bfloat16).astype(jnp.float32)
             tops[t, pl.ds(e, 1), :] = top
-            part = mag * jnp.where(top > 1e-30, 1.0 / top, 0.0)
-            root = part * lax.rsqrt(jnp.maximum(part, 1e-30))
-            code = jnp.exp2(root * SPAN - BASE)
+            weight = jnp.where(top > 1e-30, SPAN * lax.rsqrt(jnp.maximum(top, 1e-30)), 0.0)
+            root = mag * lax.rsqrt(jnp.maximum(mag, 1e-37))
+            code = jnp.exp2(root * weight - BASE)
             code = jnp.where(x < 0, -code, code)
-            turned[...] = code.T.astype(jnp.bfloat16)
+            turned[...] = code.astype(jnp.bfloat16).T
             for k in range(parts):
                 outs[k][t * height : (t + 1) * height, :] = turned[pl.ds(starts[k], height), :]
 
     @pl.when(e == count)
     def _():
-        cols = turned.shape[0]
         at = 0
         if routed:
             at = rw.shape[0]
             made = (rw[...] * gain[...]).astype(jnp.bfloat16)
+        for d in range(parts):
+            for t in range(2):
+                row = tops[t, :, d * height : (d + 1) * height]
+                sides[d, :, t * LANES : t * LANES + height] = row.astype(jnp.bfloat16)
         for k in range(parts):
             if routed:
                 outs[k][:at, :] = made
-            for t in range(2):
-                row = pltpu.roll(tops[t], cols - starts[k], 1)[:, :LANES]
-                outs[k][at : at + SIDE, t * LANES : (t + 1) * LANES] = row.astype(jnp.bfloat16)
+            outs[k][at : at + SIDE, :] = sides[me[0] ^ k]
 
 
 def pack(w_gate, w_up, routing, me, first, count, parts):
@@ -72,6 +74,7 @@
             scratch_shapes=[
                 pltpu.VMEM((cols, rows), jnp.bfloat16),
                 pltpu.VMEM((2, SIDE, cols), jnp.float32),
+                pltpu.VMEM((parts, SIDE, 2 * LANES), jnp.bfloat16),
             ],
         ),
         out_shape=[jax.ShapeDtypeStruct((length, rows), jnp.bfloat16)] * parts
@@ -105,18 +108,18 @@
             for k in range(parts):
                 refs[0][:, pl.ds(starts[k], rows)] = routes[k][...]
 
-    step = 16
+    step = height
     down = lax.broadcasted_iota(jnp.int32, (step, LANES), 0)
     across = lax.broadcasted_iota(jnp.int32, (step, LANES), 1)
     for t in range(2):
         top = jnp.concatenate([tops[t, pl.ds(k * SIDE + e, 1), :] for k in range(parts)], axis=0)
-        top = (top * (1.0 / (SPAN * SPAN))).T
+        top = (top * (1.0 / (SPAN * LN2) ** 2)).T
         scale = jnp.zeros((1, LANES), jnp.float32)
         for r in range(0, height, step):
             values, total = [], jnp.zeros((step, rows), jnp.float32)
             for k in range(parts):
                 code = bulk[k][t * height + r : t * height + r + step, :].astype(jnp.float32)
-                root = jnp.log2(jnp.abs(code)) + BASE
+                root = jnp.log(jnp.abs(code)) + BASE * LN2
                 mag = root * root * top[r : r + step, k : k + 1]
                 total = total + mag
                 values.append(jnp.where(code < 0, -mag, mag))

time: 459 us -> 431 us (0.939)
  Pallas kernels: 140 us -> 104 us
  waiting for transfers between devices: 224 us -> 243 us
  starting transfers between devices: 68.7 us -> 54.7 us
    pallas_call x9 -> x7, Pallas kernels: 76 us -> 48.9 us  [unpack(): pl.pallas_call(functools.partial(unpack_kernel, parts, first, bool(routes...]
    ppermute x63 -> x49, waiting for transfers between devices: 224 us -> 243 us  [exchanged(): moved.append(lax.ppermute(pieces[k], 'rows', pairs))]
    ppermute x63 -> x49, starting transfers between devices: 68.7 us -> 54.7 us  [exchanged(): moved.append(lax.ppermute(pieces[k], 'rows', pairs))]
    pallas_call x9 -> x7, Pallas kernels: 63.6 us -> 55.2 us  [pack(): pl.pallas_call(functools.partial(pack_kernel, parts, count, bool(routing)...]
  transfers between devices with their start and end apart: 63 -> 49, of which waited for: 24 -> 18; matrix products, arithmetic and copies ran while one was open for 0% -> 0% of each run, Pallas kernels for 17% -> 11%
where the time goes in v2:
time: 431 us; the launch traced here: 429 us
  waiting for transfers between devices  243 us (56%)
  Pallas kernels  104 us (24%)
  starting transfers between devices  54.7 us (13%)
  blocking collectives  17.2 us (4%)
  local copies, waits for them, and re-layouts  8.4 us (2%)
    ppermute x49, waiting for transfers between devices, exchanged(): moved.append(lax.ppermute(pieces[k], 'rows', pairs))  243 us
    pallas_call x7, Pallas kernels, pack(): pl.pallas_call(functools.partial(pack_kernel, parts, count, bool(routing)...  55.2 us
    ppermute x49, starting transfers between devices, exchanged(): moved.append(lax.ppermute(pieces[k], 'rows', pairs))  54.7 us
    pallas_call x7, Pallas kernels, unpack(): pl.pallas_call(functools.partial(unpack_kernel, parts, first, bool(routes...  48.9 us
    all_gather x1, blocking collectives, exchanged(): whole = lax.all_gather(part, 'owner', axis=0, tiled=True).T  17.2 us
  transfers between devices with their start and end apart: 49, of which 18 were waited for; matrix products, arithmetic and copies ran while one was open for 0% of the time, Pallas kernels for 11%

profile of v2, /device:TPU:0, one launch (start us, length us, event | category | flops | bytes accessed | tf_op | source)
XLA Modules:
  0.0 428.6 jit_solution(3428694224651275788)
XLA Ops:
  0.6 4.0 pack.7
  4.6 9.7 %pack.8 = (bf16[1192,256]{1,0:T(8,128)(2,1)}, bf16[1192,256]{1,0:T(8,128)(2,1)}, bf16[1192,256]{1,0:T(8,128)(2,1)}, bf16[1192,256]{1,0:T(8,128)(2,1)}, bf16[1192...) custom-call(s32[1]{0:T(128)} %get-tuple-element.101.me, ...), custom_call_target="tpu_custom_call" | custom-call | tf_op jit(solution)/shard_map/pack/pallas_call | solution.py:67
  14.3 12.2 %pack.9 = (bf16[1544,256]{1,0:T(8,128)(2,1)}, bf16[1544,256]{1,0:T(8,128)(2,1)}, bf16[1544,256]{1,0:T(8,128)(2,1)}, bf16[1544,256]{1,0:T(8,128)(2,1)}, bf16[1544...) custom-call(s32[1]{0:T(128)} %get-tuple-element.102.me, ...), custom_call_target="tpu_custom_call" | custom-call | tf_op jit(solution)/shard_map/pack/pallas_call | solution.py:67
  26.5 12.2 %pack.10 = (bf16[1544,256]{1,0:T(8,128)(2,1)}, bf16[1544,256]{1,0:T(8,128)(2,1)}, bf16[1544,256]{1,0:T(8,128)(2,1)}, bf16[1544,256]{1,0:T(8,128)(2,1)}, bf16[154...) custom-call(s32[1]{0:T(128)} %get-tuple-element.103.me, ...), custom_call_target="tpu_custom_call" | custom-call | tf_op jit(solution)/shard_map/pack/pallas_call | solution.py:67
  38.7 8.5 %pack.11 = (bf16[968,256]{1,0:T(8,128)(2,1)}, bf16[968,256]{1,0:T(8,128)(2,1)}, bf16[968,256]{1,0:T(8,128)(2,1)}, bf16[968,256]{1,0:T(8,128)(2,1)}, bf16[968,256...) custom-call(s32[1]{0:T(128)} %get-tuple-element.104.me, ...), custom_call_target="tpu_custom_call" | custom-call | tf_op jit(solution)/shard_map/pack/pallas_call | solution.py:67
  47.3 4.6 %pack.12 = (bf16[392,256]{1,0:T(8,128)(2,1)}, bf16[392,256]{1,0:T(8,128)(2,1)}, bf16[392,256]{1,0:T(8,128)(2,1)}, bf16[392,256]{1,0:T(8,128)(2,1)}, bf16[392,256...) custom-call(s32[1]{0:T(128)} %get-tuple-element.105.me, ...), custom_call_target="tpu_custom_call" | custom-call | tf_op jit(solution)/shard_map/pack/pallas_call | solution.py:67
  52.0 3.9 pack.13
  56.5 2.6 collective-permute-start.1
  63.7 2.5 collective-permute-start.47
  69.0 2.2 collective-permute-done.44.refs_3_.refs_11_
  74.1 7.5 %collective-permute-done.46.refs_5_.refs_13_ = bf16[392,256]{1,0:T(8,128)(2,1)S(1)} collective-permute-done((bf16[392,256]{1,0:T(8,128)(2,1)S(1)}, bf16[392,256]{1,0:T(8,128)(2,1)S(1)}, u32[]{:S(2)}, u32[]{:S(2)}) %collective-permute-start.46) | collective-permute-done | bytes 200736 | tf_op jit(solution)/shard_map/ppermute | solution.py:187
  87.5 6.8 %collective-permute-done.11.refs_5_.refs_13_ = bf16[392,256]{1,0:T(8,128)(2,1)S(1)} collective-permute-done((bf16[392,256]{1,0:T(8,128)(2,1)}, bf16[392,256]{1,0:T(8,128)(2,1)S(1)}, u32[]{:S(2)}, u32[]{:S(2)}) %collective-permute-start.11) | collective-permute-done | bytes 200736 | tf_op jit(solution)/shard_map/ppermute | solution.py:187
  96.2 20.1 %collective-permute-done.13.refs_7_.refs_15_ = bf16[392,256]{1,0:T(8,128)(2,1)S(1)} collective-permute-done((bf16[392,256]{1,0:T(8,128)(2,1)}, bf16[392,256]{1,0:T(8,128)(2,1)S(1)}, u32[]{:S(2)}, u32[]{:S(2)}) %collective-permute-start.13) | collective-permute-done | bytes 200736 | tf_op jit(solution)/shard_map/ppermute | solution.py:187
  117.8 6.6 %collective-permute-done.8.refs_2_.refs_10_ = bf16[392,256]{1,0:T(8,128)(2,1)S(1)} collective-permute-done((bf16[392,256]{1,0:T(8,128)(2,1)}, bf16[392,256]{1,0:T(8,128)(2,1)S(1)}, u32[]{:S(2)}, u32[]{:S(2)}) %collective-permute-start.8) | collective-permute-done | bytes 200736 | tf_op jit(solution)/shard_map/ppermute | solution.py:187
  133.0 26.9 %collective-permute-done.17.refs_4_.refs_12_ = bf16[968,256]{1,0:T(8,128)(2,1)S(1)} collective-permute-done((bf16[968,256]{1,0:T(8,128)(2,1)S(1)}, bf16[968,256]{1,0:T(8,128)(2,1)S(1)}, u32[]{:S(2)}, u32[]{:S(2)}) %collective-permute-start.17) | collective-permute-done | bytes 495648 | tf_op jit(solution)/shard_map/ppermute | solution.py:187
  161.1 6.1 %collective-permute-done.18.refs_5_.refs_13_ = bf16[968,256]{1,0:T(8,128)(2,1)S(1)} collective-permute-done((bf16[968,256]{1,0:T(8,128)(2,1)S(1)}, bf16[968,256]{1,0:T(8,128)(2,1)S(1)}, u32[]{:S(2)}, u32[]{:S(2)}) %collective-permute-start.18) | collective-permute-done | bytes 495648 | tf_op jit(solution)/shard_map/ppermute | solution.py:187
  175.2 9.0 %collective-permute-done.37.refs_3_.refs_11_.refs_19_ = bf16[1192,256]{1,0:T(8,128)(2,1)S(1)} collective-permute-done((bf16[1192,256]{1,0:T(8,128)(2,1)}, bf16[1192,256]{1,0:T(8,128)(2,1)S(1)}, u32[]{:S(2)}, u32[]{:S(2)}) %collective-permute-start.37) | collective-permute-done | bytes 610336 | tf_op jit(solution)/shard_map/ppermute | solution.py:187
  185.0 14.1 %collective-permute-done.38.refs_4_.refs_12_.refs_20_ = bf16[1192,256]{1,0:T(8,128)(2,1)S(1)} collective-permute-done((bf16[1192,256]{1,0:T(8,128)(2,1)}, bf16[1192,256]{1,0:T(8,128)(2,1)S(1)}, u32[]{:S(2)}, u32[]{:S(2)}) %collective-permute-start.38) | collective-permute-done | bytes 610336 | tf_op jit(solution)/shard_map/ppermute | solution.py:187
  199.1 12.0 %collective-permute-done.39.refs_5_.refs_13_.refs_21_ = bf16[1192,256]{1,0:T(8,128)(2,1)S(1)} collective-permute-done((bf16[1192,256]{1,0:T(8,128)(2,1)}, bf16[1192,256]{1,0:T(8,128)(2,1)S(1)}, u32[]{:S(2)}, u32[]{:S(2)}) %collective-permute-start.39) | collective-permute-done | bytes 610336 | tf_op jit(solution)/shard_map/ppermute | solution.py:187
  214.2 30.7 %collective-permute-done.41.refs_7_.refs_15_.refs_23_ = bf16[1192,256]{1,0:T(8,128)(2,1)} collective-permute-done((bf16[1192,256]{1,0:T(8,128)(2,1)}, bf16[1192,256]{1,0:T(8,128)(2,1)}, u32[]{:S(2)}, u32[]{:S(2)}) %collective-permute-start.41) | collective-permute-done | bytes 610336 | tf_op jit(solution)/shard_map/ppermute | solution.py:187
  249.4 48.4 %collective-permute-done.32.refs_5_.refs_13_ = bf16[1544,256]{1,0:T(8,128)(2,1)} collective-permute-done((bf16[1544,256]{1,0:T(8,128)(2,1)}, bf16[1544,256]{1,0:T(8,128)(2,1)}, u32[]{:S(2)}, u32[]{:S(2)}) %collective-permute-start.32) | collective-permute-done | bytes 790560 | tf_op jit(solution)/shard_map/ppermute | solution.py:187
  304.1 3.9 unpack.7
  308.1 8.8 %unpack.8 = (bf16[32,96,2048]{2,1,0:T(8,128)(2,1)}, bf16[32,96,2048]{2,1,0:T(8,128)(2,1)}, f32[32,96]{1,0:T(8,128)}, f32[32,96]{1,0:T(8,128)}, bf16[32,2048]{1,0:T(8,128)(2,1)}) custom-call(s32[1]{0:T(128)} %bitcast.me, ...), custom_call_target="tpu_custom_call", output_to_operand_aliasing={{0}: (25, {}), {1}: (26, {}), {2}: (27, {}), {3}: (28, {})} | custom-call | tf_op jit(solution)/shard_map/unpack/pallas_call | solution.py:162
  318.1 2.2 collective-permute-start.2
  320.3 34.2 %collective-permute-done.24.refs_4_.refs_12_ = bf16[1544,256]{1,0:T(8,128)(2,1)} collective-permute-done((bf16[1544,256]{1,0:T(8,128)(2,1)}, bf16[1544,256]{1,0:T(8,128)(2,1)}, u32[]{:S(2)}, u32[]{:S(2)}) %collective-permute-start.24) | collective-permute-done | bytes 790560 | tf_op jit(solution)/shard_map/ppermute | solution.py:187
  354.9 14.5 %collective-permute-done.25.refs_5_.refs_13_ = bf16[1544,256]{1,0:T(8,128)(2,1)} collective-permute-done((bf16[1544,256]{1,0:T(8,128)(2,1)}, bf16[1544,256]{1,0:T(8,128)(2,1)}, u32[]{:S(2)}, u32[]{:S(2)}) %collective-permute-start.25) | collective-permute-done | bytes 790560 | tf_op jit(solution)/shard_map/ppermute | solution.py:187
  373.3 17.2 %all_gather.3 = bf16[128,2048]{1,0:T(8,128)(2,1)S(1)} all-gather(bf16[32,2048]{1,0:T(8,128)(2,1)} %get-tuple-element.171), channel_id=1, replica_groups=mesh['owner'=4,'rows'=8] {'owner'}, dimensions={0}, use_global_device_ids=true | all-gather | bytes 655360 | tf_op jit(solution)/shard_map/all_gather | solution.py:196
  391.6 10.8 %unpack.9 = (bf16[32,96,2048]{2,1,0:T(8,128)(2,1)}, bf16[32,96,2048]{2,1,0:T(8,128)(2,1)}, f32[32,96]{1,0:T(8,128)}, f32[32,96]{1,0:T(8,128)}) custom-call(s32[1]{0:T(128)} %bitcast.me, bf16[1544,256]{1,0:T(8,128)(2,1)} %get-tuple-element.139.refs_0_.refs_8_, ...), custom_call_target="tpu_custom_call", output_to_operand_aliasing={{0}: (17, {}), {1}: (18, {}), {2}: (19, {}), {3}: (20, {})} | custom-call | tf_op jit(solution)/shard_map/unpack/pallas_call | solution.py:162
  402.4 10.8 %unpack.10 = (bf16[32,96,2048]{2,1,0:T(8,128)(2,1)}, bf16[32,96,2048]{2,1,0:T(8,128)(2,1)}, f32[32,96]{1,0:T(8,128)}, f32[32,96]{1,0:T(8,128)}) custom-call(s32[1]{0:T(128)} %bitcast.me, bf16[1544,256]{1,0:T(8,128)(2,1)} %get-tuple-element.131.refs_0_.refs_8_, ...), custom_call_target="tpu_custom_call", output_to_operand_aliasing={{0}: (17, {}), {1}: (18, {}), {2}: (19, {}), {3}: (20, {})} | custom-call | tf_op jit(solution)/shard_map/unpack/pallas_call | solution.py:162
  413.2 7.6 %unpack.11 = (bf16[32,96,2048]{2,1,0:T(8,128)(2,1)}, bf16[32,96,2048]{2,1,0:T(8,128)(2,1)}, f32[32,96]{1,0:T(8,128)}, f32[32,96]{1,0:T(8,128)}) custom-call(s32[1]{0:T(128)} %bitcast.me, bf16[968,256]{1,0:T(8,128)(2,1)} %get-tuple-element.123.refs_0_.refs_8_, ...), custom_call_target="tpu_custom_call", output_to_operand_aliasing={{0}: (17, {}), {1}: (18, {}), {2}: (19, {}), {3}: (20, {})} | custom-call | tf_op jit(solution)/shard_map/unpack/pallas_call | solution.py:162
  420.8 4.0 unpack.12
  425.6 2.9 unpack.13
  (162 shorter events, 59.9 us)
Async XLA Ops:
  73.5 20.8 %collective-permute-start.11 = (bf16[392,256]{1,0:T(8,128)(2,1)}, bf16[392,256]{1,0:T(8,128)(2,1)S(1)}, u32[]{:S(2)}, u32[]{:S(2)}) collective-permute-start(bf16[392,256]{1,0:T(8,128)(2,1)} %get-tuple-element.120), channel_id=1, source_target_pairs={{0,5},{1,4},{2,7},{3,6},{4,1},{5,0},{6,3},{7,2},{8,13},{9,12},{10,... | collective-permute-start | bytes 602120 | tf_op jit(solution)/shard_map/ppermute | solution.py:187
  83.6 46.2 %collective-permute-start.14 = (bf16[968,256]{1,0:T(8,128)(2,1)}, bf16[968,256]{1,0:T(8,128)(2,1)S(1)}, u32[]{:S(2)}, u32[]{:S(2)}) collective-permute-start(bf16[968,256]{1,0:T(8,128)(2,1)} %get-tuple-element.124), channel_id=1, source_target_pairs={{0,1},{1,0},{2,3},{3,2},{4,5},{5,4},{6,7},{7,6},{8,9},{9,8},{10,11... | collective-permute-start | bytes 1486856 | tf_op jit(solution)/shard_map/ppermute | solution.py:187
  84.3 45.7 %collective-permute-start.15 = (bf16[968,256]{1,0:T(8,128)(2,1)}, bf16[968,256]{1,0:T(8,128)(2,1)S(1)}, u32[]{:S(2)}, u32[]{:S(2)}) collective-permute-start(bf16[968,256]{1,0:T(8,128)(2,1)} %get-tuple-element.125), channel_id=1, source_target_pairs={{0,2},{1,3},{2,0},{3,1},{4,6},{5,7},{6,4},{7,5},{8,10},{9,11},{10,... | collective-permute-start | bytes 1486856 | tf_op jit(solution)/shard_map/ppermute | solution.py:187
  87.5 44.5 %collective-permute-start.16 = (bf16[968,256]{1,0:T(8,128)(2,1)S(1)}, bf16[968,256]{1,0:T(8,128)(2,1)S(1)}, u32[]{:S(2)}, u32[]{:S(2)}) collective-permute-start(bf16[968,256]{1,0:T(8,128)(2,1)S(1)} %copy-done.37), channel_id=1, source_target_pairs={{0,3},{1,2},{2,1},{3,0},{4,7},{5,6},{6,5},{7,4},{8,11},{9,10},{10,... | collective-permute-start | bytes 1486856 | tf_op jit(solution)/shard_map/ppermute | solution.py:187
  94.4 22.0 %collective-permute-start.13 = (bf16[392,256]{1,0:T(8,128)(2,1)}, bf16[392,256]{1,0:T(8,128)(2,1)S(1)}, u32[]{:S(2)}, u32[]{:S(2)}) collective-permute-start(bf16[392,256]{1,0:T(8,128)(2,1)} %get-tuple-element.122), channel_id=1, source_target_pairs={{0,7},{1,6},{2,5},{3,4},{4,3},{5,2},{6,1},{7,0},{8,15},{9,14},{10,... | collective-permute-start | bytes 602120 | tf_op jit(solution)/shard_map/ppermute | solution.py:187
  124.4 35.4 %collective-permute-start.17 = (bf16[968,256]{1,0:T(8,128)(2,1)S(1)}, bf16[968,256]{1,0:T(8,128)(2,1)S(1)}, u32[]{:S(2)}, u32[]{:S(2)}) collective-permute-start(bf16[968,256]{1,0:T(8,128)(2,1)S(1)} %copy-done.36), channel_id=1, source_target_pairs={{0,4},{1,5},{2,6},{3,7},{4,0},{5,1},{6,2},{7,3},{8,12},{9,13},{10,... | collective-permute-start | bytes 1486856 | tf_op jit(solution)/shard_map/ppermute | solution.py:187
  127.7 39.5 %collective-permute-start.18 = (bf16[968,256]{1,0:T(8,128)(2,1)S(1)}, bf16[968,256]{1,0:T(8,128)(2,1)S(1)}, u32[]{:S(2)}, u32[]{:S(2)}) collective-permute-start(bf16[968,256]{1,0:T(8,128)(2,1)S(1)} %copy-done.35), channel_id=1, source_target_pairs={{0,5},{1,4},{2,7},{3,6},{4,1},{5,0},{6,3},{7,2},{8,13},{9,12},{10,... | collective-permute-start | bytes 1486856 | tf_op jit(solution)/shard_map/ppermute | solution.py:187
  129.8 39.1 %collective-permute-start.19 = (bf16[968,256]{1,0:T(8,128)(2,1)S(1)}, bf16[968,256]{1,0:T(8,128)(2,1)S(1)}, u32[]{:S(2)}, u32[]{:S(2)}) collective-permute-start(bf16[968,256]{1,0:T(8,128)(2,1)S(1)} %copy-done.34), channel_id=1, source_target_pairs={{0,6},{1,7},{2,4},{3,5},{4,2},{5,3},{6,0},{7,1},{8,14},{9,15},{10,... | collective-permute-start | bytes 1486856 | tf_op jit(solution)/shard_map/ppermute | solution.py:187
  129.9 41.5 %collective-permute-start.20 = (bf16[968,256]{1,0:T(8,128)(2,1)S(1)}, bf16[968,256]{1,0:T(8,128)(2,1)S(1)}, u32[]{:S(2)}, u32[]{:S(2)}) collective-permute-start(bf16[968,256]{1,0:T(8,128)(2,1)S(1)} %copy-done.33), channel_id=1, source_target_pairs={{0,7},{1,6},{2,5},{3,4},{4,3},{5,2},{6,1},{7,0},{8,15},{9,14},{10,... | collective-permute-start | bytes 1486856 | tf_op jit(solution)/shard_map/ppermute | solution.py:187
  132.0 40.3 %collective-permute-start.35 = (bf16[1192,256]{1,0:T(8,128)(2,1)}, bf16[1192,256]{1,0:T(8,128)(2,1)S(1)}, u32[]{:S(2)}, u32[]{:S(2)}) collective-permute-start(bf16[1192,256]{1,0:T(8,128)(2,1)} %get-tuple-element.148), channel_id=1, source_target_pairs={{0,1},{1,0},{2,3},{3,2},{4,5},{5,4},{6,7},{7,6},{8,9},{9,8},{10,11... | collective-permute-start | bytes 1830920 | tf_op jit(solution)/shard_map/ppermute | solution.py:187
  169.7 29.3 %collective-permute-start.38 = (bf16[1192,256]{1,0:T(8,128)(2,1)}, bf16[1192,256]{1,0:T(8,128)(2,1)S(1)}, u32[]{:S(2)}, u32[]{:S(2)}) collective-permute-start(bf16[1192,256]{1,0:T(8,128)(2,1)} %get-tuple-element.151), channel_id=1, source_target_pairs={{0,4},{1,5},{2,6},{3,7},{4,0},{5,1},{6,2},{7,3},{8,12},{9,13},{10,... | collective-permute-start | bytes 1830920 | tf_op jit(solution)/shard_map/ppermute | solution.py:187
  172.3 38.8 %collective-permute-start.39 = (bf16[1192,256]{1,0:T(8,128)(2,1)}, bf16[1192,256]{1,0:T(8,128)(2,1)S(1)}, u32[]{:S(2)}, u32[]{:S(2)}) collective-permute-start(bf16[1192,256]{1,0:T(8,128)(2,1)} %get-tuple-element.152), channel_id=1, source_target_pairs={{0,5},{1,4},{2,7},{3,6},{4,1},{5,0},{6,3},{7,2},{8,13},{9,12},{10,... | collective-permute-start | bytes 1830920 | tf_op jit(solution)/shard_map/ppermute | solution.py:187
  172.3 40.2 %collective-permute-start.40 = (bf16[1192,256]{1,0:T(8,128)(2,1)}, bf16[1192,256]{1,0:T(8,128)(2,1)}, u32[]{:S(2)}, u32[]{:S(2)}) collective-permute-start(bf16[1192,256]{1,0:T(8,128)(2,1)} %get-tuple-element.153), channel_id=1, source_target_pairs={{0,6},{1,7},{2,4},{3,5},{4,2},{5,3},{6,0},{7,1},{8,14},{9,15},{10,... | collective-permute-start | bytes 1830920 | tf_op jit(solution)/shard_map/ppermute | solution.py:187
  173.7 72.2 %collective-permute-start.28 = (bf16[1544,256]{1,0:T(8,128)(2,1)}, bf16[1544,256]{1,0:T(8,128)(2,1)}, u32[]{:S(2)}, u32[]{:S(2)}) collective-permute-start(bf16[1544,256]{1,0:T(8,128)(2,1)} %get-tuple-element.140), channel_id=1, source_target_pairs={{0,1},{1,0},{2,3},{3,2},{4,5},{5,4},{6,7},{7,6},{8,9},{9,8},{10,11... | collective-permute-start | bytes 2371592 | tf_op jit(solution)/shard_map/ppermute | solution.py:187
  184.2 63.2 %collective-permute-start.29 = (bf16[1544,256]{1,0:T(8,128)(2,1)}, bf16[1544,256]{1,0:T(8,128)(2,1)}, u32[]{:S(2)}, u32[]{:S(2)}) collective-permute-start(bf16[1544,256]{1,0:T(8,128)(2,1)} %get-tuple-element.141), channel_id=1, source_target_pairs={{0,2},{1,3},{2,0},{3,1},{4,6},{5,7},{6,4},{7,5},{8,10},{9,11},{10,... | collective-permute-start | bytes 2371592 | tf_op jit(solution)/shard_map/ppermute | solution.py:187
  199.1 49.1 %collective-permute-start.30 = (bf16[1544,256]{1,0:T(8,128)(2,1)}, bf16[1544,256]{1,0:T(8,128)(2,1)}, u32[]{:S(2)}, u32[]{:S(2)}) collective-permute-start(bf16[1544,256]{1,0:T(8,128)(2,1)} %get-tuple-element.142), channel_id=1, source_target_pairs={{0,3},{1,2},{2,1},{3,0},{4,7},{5,6},{6,5},{7,4},{8,11},{9,10},{10,... | collective-permute-start | bytes 2371592 | tf_op jit(solution)/shard_map/ppermute | solution.py:187
  211.1 37.8 %collective-permute-start.31 = (bf16[1544,256]{1,0:T(8,128)(2,1)}, bf16[1544,256]{1,0:T(8,128)(2,1)}, u32[]{:S(2)}, u32[]{:S(2)}) collective-permute-start(bf16[1544,256]{1,0:T(8,128)(2,1)} %get-tuple-element.143), channel_id=1, source_target_pairs={{0,4},{1,5},{2,6},{3,7},{4,0},{5,1},{6,2},{7,3},{8,12},{9,13},{10,... | collective-permute-start | bytes 2371592 | tf_op jit(solution)/shard_map/ppermute | solution.py:187
  212.5 32.3 %collective-permute-start.41 = (bf16[1192,256]{1,0:T(8,128)(2,1)}, bf16[1192,256]{1,0:T(8,128)(2,1)}, u32[]{:S(2)}, u32[]{:S(2)}) collective-permute-start(bf16[1192,256]{1,0:T(8,128)(2,1)} %get-tuple-element.154), channel_id=1, source_target_pairs={{0,7},{1,6},{2,5},{3,4},{4,3},{5,2},{6,1},{7,0},{8,15},{9,14},{10,... | collective-permute-start | bytes 1830920 | tf_op jit(solution)/shard_map/ppermute | solution.py:187
  244.8 52.9 %collective-permute-start.32 = (bf16[1544,256]{1,0:T(8,128)(2,1)}, bf16[1544,256]{1,0:T(8,128)(2,1)}, u32[]{:S(2)}, u32[]{:S(2)}) collective-permute-start(bf16[1544,256]{1,0:T(8,128)(2,1)} %get-tuple-element.144), channel_id=1, source_target_pairs={{0,5},{1,4},{2,7},{3,6},{4,1},{5,0},{6,3},{7,2},{8,13},{9,12},{10,... | collective-permute-start | bytes 2371592 | tf_op jit(solution)/shard_map/ppermute | solution.py:187
  245.9 53.9 %collective-permute-start.33 = (bf16[1544,256]{1,0:T(8,128)(2,1)}, bf16[1544,256]{1,0:T(8,128)(2,1)}, u32[]{:S(2)}, u32[]{:S(2)}) collective-permute-start(bf16[1544,256]{1,0:T(8,128)(2,1)} %get-tuple-element.145), channel_id=1, source_target_pairs={{0,6},{1,7},{2,4},{3,5},{4,2},{5,3},{6,0},{7,1},{8,14},{9,15},{10,... | collective-permute-start | bytes 2371592 | tf_op jit(solution)/shard_map/ppermute | solution.py:187
  247.4 52.8 %collective-permute-start.34 = (bf16[1544,256]{1,0:T(8,128)(2,1)}, bf16[1544,256]{1,0:T(8,128)(2,1)}, u32[]{:S(2)}, u32[]{:S(2)}) collective-permute-start(bf16[1544,256]{1,0:T(8,128)(2,1)} %get-tuple-element.146), channel_id=1, source_target_pairs={{0,7},{1,6},{2,5},{3,4},{4,3},{5,2},{6,1},{7,0},{8,15},{9,14},{10,... | collective-permute-start | bytes 2371592 | tf_op jit(solution)/shard_map/ppermute | solution.py:187
  248.2 52.6 %collective-permute-start.21 = (bf16[1544,256]{1,0:T(8,128)(2,1)}, bf16[1544,256]{1,0:T(8,128)(2,1)}, u32[]{:S(2)}, u32[]{:S(2)}) collective-permute-start(bf16[1544,256]{1,0:T(8,128)(2,1)} %get-tuple-element.132), channel_id=1, source_target_pairs={{0,1},{1,0},{2,3},{3,2},{4,5},{5,4},{6,7},{7,6},{8,9},{9,8},{10,11... | collective-permute-start | bytes 2371592 | tf_op jit(solution)/shard_map/ppermute | solution.py:187
  248.9 53.4 %collective-permute-start.22 = (bf16[1544,256]{1,0:T(8,128)(2,1)}, bf16[1544,256]{1,0:T(8,128)(2,1)}, u32[]{:S(2)}, u32[]{:S(2)}) collective-permute-start(bf16[1544,256]{1,0:T(8,128)(2,1)} %get-tuple-element.133), channel_id=1, source_target_pairs={{0,2},{1,3},{2,0},{3,1},{4,6},{5,7},{6,4},{7,5},{8,10},{9,11},{10,... | collective-permute-start | bytes 2371592 | tf_op jit(solution)/shard_map/ppermute | solution.py:187
  299.7 54.7 %collective-permute-start.24 = (bf16[1544,256]{1,0:T(8,128)(2,1)}, bf16[1544,256]{1,0:T(8,128)(2,1)}, u32[]{:S(2)}, u32[]{:S(2)}) collective-permute-start(bf16[1544,256]{1,0:T(8,128)(2,1)} %get-tuple-element.135), channel_id=1, source_target_pairs={{0,4},{1,5},{2,6},{3,7},{4,0},{5,1},{6,2},{7,3},{8,12},{9,13},{10,... | collective-permute-start | bytes 2371592 | tf_op jit(solution)/shard_map/ppermute | solution.py:187
  300.2 69.2 %collective-permute-start.25 = (bf16[1544,256]{1,0:T(8,128)(2,1)}, bf16[1544,256]{1,0:T(8,128)(2,1)}, u32[]{:S(2)}, u32[]{:S(2)}) collective-permute-start(bf16[1544,256]{1,0:T(8,128)(2,1)} %get-tuple-element.136), channel_id=1, source_target_pairs={{0,5},{1,4},{2,7},{3,6},{4,1},{5,0},{6,3},{7,2},{8,13},{9,12},{10,... | collective-permute-start | bytes 2371592 | tf_op jit(solution)/shard_map/ppermute | solution.py:187
  300.8 70.4 %collective-permute-start.26 = (bf16[1544,256]{1,0:T(8,128)(2,1)}, bf16[1544,256]{1,0:T(8,128)(2,1)}, u32[]{:S(2)}, u32[]{:S(2)}) collective-permute-start(bf16[1544,256]{1,0:T(8,128)(2,1)} %get-tuple-element.137), channel_id=1, source_target_pairs={{0,6},{1,7},{2,4},{3,5},{4,2},{5,3},{6,0},{7,1},{8,14},{9,15},{10,... | collective-permute-start | bytes 2371592 | tf_op jit(solution)/shard_map/ppermute | solution.py:187
  302.3 70.4 %collective-permute-start.27 = (bf16[1544,256]{1,0:T(8,128)(2,1)}, bf16[1544,256]{1,0:T(8,128)(2,1)}, u32[]{:S(2)}, u32[]{:S(2)}) collective-permute-start(bf16[1544,256]{1,0:T(8,128)(2,1)} %get-tuple-element.138), channel_id=1, source_target_pairs={{0,7},{1,6},{2,5},{3,4},{4,3},{5,2},{6,1},{7,0},{8,15},{9,14},{10,... | collective-permute-start | bytes 2371592 | tf_op jit(solution)/shard_map/ppermute | solution.py:187
  318.1 106.7 %collective-permute-start.2 = (bf16[200,256]{1,0:T(8,128)(2,1)}, bf16[200,256]{1,0:T(8,128)(2,1)S(1)}, u32[]{:S(2)}, u32[]{:S(2)}) collective-permute-start(bf16[200,256]{1,0:T(8,128)(2,1)} %get-tuple-element.110), channel_id=1, source_target_pairs={{0,3},{1,2},{2,1},{3,0},{4,7},{5,6},{6,5},{7,4},{8,11},{9,10},{10,... | collective-permute-start | bytes 307208 | tf_op jit(solution)/shard_map/ppermute | solution.py:187
  354.4 70.4 %collective-permute-start.3 = (bf16[200,256]{1,0:T(8,128)(2,1)}, bf16[200,256]{1,0:T(8,128)(2,1)S(1)}, u32[]{:S(2)}, u32[]{:S(2)}) collective-permute-start(bf16[200,256]{1,0:T(8,128)(2,1)} %get-tuple-element.111), channel_id=1, source_target_pairs={{0,4},{1,5},{2,6},{3,7},{4,0},{5,1},{6,2},{7,3},{8,12},{9,13},{10,... | collective-permute-start | bytes 307208 | tf_op jit(solution)/shard_map/ppermute | solution.py:187
  369.3 55.5 %collective-permute-start.4 = (bf16[200,256]{1,0:T(8,128)(2,1)}, bf16[200,256]{1,0:T(8,128)(2,1)S(1)}, u32[]{:S(2)}, u32[]{:S(2)}) collective-permute-start(bf16[200,256]{1,0:T(8,128)(2,1)} %get-tuple-element.112), channel_id=1, source_target_pairs={{0,5},{1,4},{2,7},{3,6},{4,1},{5,0},{6,3},{7,2},{8,13},{9,12},{10,... | collective-permute-start | bytes 307208 | tf_op jit(solution)/shard_map/ppermute | solution.py:187
  371.2 53.6 %collective-permute-start.5 = (bf16[200,256]{1,0:T(8,128)(2,1)}, bf16[200,256]{1,0:T(8,128)(2,1)S(1)}, u32[]{:S(2)}, u32[]{:S(2)}) collective-permute-start(bf16[200,256]{1,0:T(8,128)(2,1)} %get-tuple-element.113), channel_id=1, source_target_pairs={{0,6},{1,7},{2,4},{3,5},{4,2},{5,3},{6,0},{7,1},{8,14},{9,15},{10,... | collective-permute-start | bytes 307208 | tf_op jit(solution)/shard_map/ppermute | solution.py:187
  372.8 52.1 %collective-permute-start.6 = (bf16[200,256]{1,0:T(8,128)(2,1)}, bf16[200,256]{1,0:T(8,128)(2,1)S(1)}, u32[]{:S(2)}, u32[]{:S(2)}) collective-permute-start(bf16[200,256]{1,0:T(8,128)(2,1)} %get-tuple-element.114), channel_id=1, source_target_pairs={{0,7},{1,6},{2,5},{3,4},{4,3},{5,2},{6,1},{7,0},{8,15},{9,14},{10,... | collective-permute-start | bytes 307208 | tf_op jit(solution)/shard_map/ppermute | solution.py:187
  (57 other events, 2258.5 us)
